TPU v7x, 8 devices: a whole 2x2x1 slice. The times are simulated.
8 devices in a mesh: dp: 2 (over z, y), sp: 4 (over x, core).
Axes of the slice: x: 2, y: 2, z: 1, core: 2. Of those that a mesh axis runs over, the one named last changes fastest.
Arguments:
- hidden: bfloat16 [6, 1024, 3072], P('dp', 'sp'), parts along dimension 0
- norm_w: bfloat16 [3072], replicated
- w_qkv: bfloat16 [3072, 9216], replicated
- w_out: bfloat16 [32, 96, 3072], replicated
- long_factor: float32 [48], replicated
- grad_out: bfloat16 [6, 1024, 3072], P('dp', 'sp'), parts along dimension 0
Outputs:
- output 1: bfloat16 [6, 1024, 3072], P('dp', 'sp'), parts along dimension 0
- output 2: bfloat16 [6, 1024, 3072], P('dp', 'sp'), parts along dimension 0
- output 3: float32 [6144, 9216], P('dp'), parts along dimension 0
- output 4: float32 [64, 96, 3072], P('dp'), parts along dimension 0
- output 5: float32 [6144], P('dp'), parts along dimension 0
There are 2 independent parts. A program takes and returns all parts, laid end to end along the dimension named above; an argument that names none is the same for every part.
All inputs are finite; a program needn't handle non-finite values.
Results may differ from a plain program's by a relative error of at most 0.011499.
Values are sent between devices in bfloat16 or wider.
A program may use at most 1 GiB of HBM per device.

v0:
```python
import math
import functools
import jax
import jax.numpy as jnp
from jax import lax
from jax.sharding import PartitionSpec as P, NamedSharding

NORM_EPS = 1e-5
ROPE_BASE = 10000.0
ROPE_GAIN = math.sqrt(1.0 + math.log(32.0) / math.log(4096.0))
MASK_VALUE = -1e30


def rope_tables(positions, long_factor):
    half_rot = long_factor.shape[0]
    exponent = jnp.arange(half_rot, dtype=jnp.float32) / half_rot
    inv_freq = 1.0 / (long_factor * jnp.power(ROPE_BASE, exponent))
    angles = positions.astype(jnp.float32)[:, None] * inv_freq[None, :]
    return jnp.cos(angles) * ROPE_GAIN, jnp.sin(angles) * ROPE_GAIN


def rotate(head_vals, cos_t, sin_t, direction):
    half_rot = cos_t.shape[1]
    cos_b = cos_t[None, :, None, :]
    sin_b = sin_t[None, :, None, :] * direction
    first_half = head_vals[..., :half_rot]
    second_half = head_vals[..., half_rot:2 * half_rot]
    rest_dims = head_vals[..., 2 * half_rot:].astype(jnp.float32)
    return jnp.concatenate([first_half * cos_b - second_half * sin_b, second_half * cos_b + first_half * sin_b, rest_dims], axis=-1)


def norm_forward(hidden, norm_w):
    hidden_f = hidden.astype(jnp.float32)
    inv_rms = lax.rsqrt(jnp.mean(hidden_f * hidden_f, axis=-1, keepdims=True) + NORM_EPS)
    unit_rows = hidden_f * inv_rms
    return (unit_rows * norm_w.astype(jnp.float32)).astype(jnp.bfloat16), unit_rows, inv_rms


def norm_backward(grad_normed, unit_rows, inv_rms, norm_w):
    grad_unit = grad_normed * norm_w.astype(jnp.float32)
    mean_dot = jnp.mean(grad_unit * unit_rows, axis=-1, keepdims=True)
    return inv_rms * (grad_unit - unit_rows * mean_dot)


def split_fused(fused_qkv, n_heads, kv_heads, head_dim, cos_t, sin_t):
    n_batch, tok_len = fused_qkv.shape[0], fused_qkv.shape[1]
    q_width = n_heads * head_dim
    kv_width = kv_heads * head_dim
    queries = fused_qkv[..., :q_width].reshape(n_batch, tok_len, n_heads, head_dim)
    key_vals = fused_qkv[..., q_width:q_width + kv_width].reshape(n_batch, tok_len, kv_heads, head_dim)
    value_vals = fused_qkv[..., q_width + kv_width:].reshape(n_batch, tok_len, kv_heads, head_dim)
    return (rotate(queries, cos_t, sin_t, 1.0).astype(jnp.bfloat16), rotate(key_vals, cos_t, sin_t, 1.0).astype(jnp.bfloat16), value_vals.astype(jnp.bfloat16))


def merge_grads(grad_q, grad_k, grad_v, cos_t, sin_t):
    n_batch, tok_len = grad_q.shape[0], grad_q.shape[1]
    return jnp.concatenate([
        rotate(grad_q, cos_t, sin_t, -1.0).reshape(n_batch, tok_len, -1),
        rotate(grad_k, cos_t, sin_t, -1.0).reshape(n_batch, tok_len, -1),
        grad_v.astype(jnp.float32).reshape(n_batch, tok_len, -1)], axis=-1).astype(jnp.bfloat16)


def causal_probs(queries, key_vals):
    seq_len, head_dim = queries.shape[1], queries.shape[-1]
    scores = jnp.einsum('bqkge,bske->bkgqs', queries, key_vals, preferred_element_type=jnp.float32) * (head_dim ** -0.5)
    causal = jnp.arange(seq_len)[:, None] >= jnp.arange(seq_len)[None, :]
    return jax.nn.softmax(jnp.where(causal, scores, MASK_VALUE), axis=-1)


def attention_forward(queries, key_vals, value_vals):
    prob_mat = causal_probs(queries, key_vals)
    return jnp.einsum('bkgqs,bske->bqkge', prob_mat.astype(jnp.bfloat16), value_vals, preferred_element_type=jnp.float32).astype(jnp.bfloat16)


def attention_backward(queries, key_vals, value_vals, grad_attn):
    head_dim = queries.shape[-1]
    prob_mat = causal_probs(queries, key_vals)
    grad_v = jnp.einsum('bkgqs,bqkge->bske', prob_mat.astype(jnp.bfloat16), grad_attn, preferred_element_type=jnp.float32)
    grad_p = jnp.einsum('bqkge,bske->bkgqs', grad_attn, value_vals, preferred_element_type=jnp.float32)
    row_dot = jnp.sum(grad_p * prob_mat, axis=-1, keepdims=True)
    grad_s = (prob_mat * (grad_p - row_dot) * (head_dim ** -0.5)).astype(jnp.bfloat16)
    grad_q = jnp.einsum('bkgqs,bske->bqkge', grad_s, key_vals, preferred_element_type=jnp.float32)
    grad_k = jnp.einsum('bkgqs,bqkge->bske', grad_s, queries, preferred_element_type=jnp.float32)
    return grad_q.astype(jnp.bfloat16), grad_k.astype(jnp.bfloat16), grad_v.astype(jnp.bfloat16)


def solution(mesh):
    group_devs = mesh.shape['sp']
    to_heads = functools.partial(lax.all_to_all, axis_name='sp', split_axis=2, concat_axis=1, tiled=True)
    to_tokens = functools.partial(lax.all_to_all, axis_name='sp', split_axis=1, concat_axis=2, tiled=True)

    def device_step(hidden, norm_w, w_qkv, w_out, long_factor, grad_out):
        n_batch, tok_len = hidden.shape[0], hidden.shape[1]
        n_heads, head_dim = w_out.shape[0], w_out.shape[1]
        kv_heads = (w_qkv.shape[1] // head_dim - n_heads) // 2
        seq_len = tok_len * group_devs
        heads_local = n_heads // group_devs
        kv_local = kv_heads // group_devs
        head_shape = (n_batch, seq_len, kv_local, n_heads // kv_heads, head_dim)
        positions = lax.axis_index('sp') * tok_len + jnp.arange(tok_len)
        cos_t, sin_t = rope_tables(positions, long_factor)
        normed, unit_rows, inv_rms = norm_forward(hidden, norm_w)
        fused_qkv = jnp.einsum('btd,dw->btw', normed, w_qkv, preferred_element_type=jnp.float32)
        q_local, k_local, v_local = split_fused(fused_qkv, n_heads, kv_heads, head_dim, cos_t, sin_t)
        q_heads = to_heads(q_local).reshape(head_shape)
        k_heads = to_heads(k_local)
        v_heads = to_heads(v_local)
        attn_heads = attention_forward(q_heads, k_heads, v_heads)
        attn_local = to_tokens(attn_heads.reshape(n_batch, seq_len, heads_local, head_dim))
        projected = jnp.einsum('bthe,hed->btd', attn_local, w_out, preferred_element_type=jnp.float32)
        block_out = (hidden.astype(jnp.float32) + projected).astype(jnp.bfloat16)

        grad_w_out = jnp.einsum('bthe,btd->hed', attn_local, grad_out, preferred_element_type=jnp.float32)
        grad_attn = jnp.einsum('btd,hed->bthe', grad_out, w_out, preferred_element_type=jnp.float32).astype(jnp.bfloat16)
        grad_attn_heads = to_heads(grad_attn).reshape(head_shape)
        grad_q, grad_k, grad_v = attention_backward(q_heads, k_heads, v_heads, grad_attn_heads)
        grad_q_local = to_tokens(grad_q.reshape(n_batch, seq_len, heads_local, head_dim))
        grad_fused = merge_grads(grad_q_local, to_tokens(grad_k), to_tokens(grad_v), cos_t, sin_t)
        grad_w_qkv = jnp.einsum('btd,btw->dw', normed, grad_fused, preferred_element_type=jnp.float32)
        grad_normed = jnp.einsum('btw,dw->btd', grad_fused, w_qkv, preferred_element_type=jnp.float32)
        grad_hidden = (grad_out.astype(jnp.float32) + norm_backward(grad_normed, unit_rows, inv_rms, norm_w)).astype(jnp.bfloat16)
        grad_norm_w = jnp.sum(grad_normed * unit_rows, axis=(0, 1))
        return (block_out, grad_hidden, lax.psum(grad_w_qkv, 'sp'), lax.psum(grad_w_out, 'sp'), lax.psum(grad_norm_w, 'sp'))

    tok_spec = P('dp', 'sp', None)
    return jax.shard_map(device_step, mesh=mesh,
                         in_specs=(tok_spec, P(), P(), P(), P(), tok_spec),
                         out_specs=(tok_spec, tok_spec, P('dp', None), P('dp', None, None), P('dp')),
                         check_vma=False)
```

profile of v0, /device:TPU:0, one launch (start us, length us, event | category | flops | bytes accessed | tf_op | source)
XLA Modules:
  0.0 3328.3 jit_solution(4276142446037177413)
XLA Ops:
  11.2 52.5 %fusion.9 = f32[3,256,9216]{2,1,0:T(8,128)} fusion(bf16[3072,9216]{1,0:T(8,128)(2,1)} %param.8, bf16[3,256,3072]{2,1,0:T(8,128)(2,1)} %param.6, f32[3072]{0:T(1024)S(1)} %convert_element_type.102, f32[3,256]{1,0:T(4,128)S(1)} %add_rsqrt_fusion), kind=kOutput, calls=%fused_computation.14 | convolution fusion | flops 43495981056 | bytes 89668608 | tf_op jit(solution)/shard_map/btd,dw->btw/dot_general | solution.py:103
  86.7 12.7 fusion.64
  150.8 48.9 %all-to-all-done.1 = bf16[3,256,32,96]{1,3,0,2:T(8,128)(2,1)} async-done(((bf16[3,256,32,96]{1,3,0,2:T(8,128)(2,1)}), bf16[3,256,32,96]{1,3,0,2:T(8,128)(2,1)}, u32[]{:S(2)}, u32[]{:S(2)}) %all-to-all-start.1) | async-done | bytes 4718624 | tf_op jit(solution)/shard_map/all_to_all | solution.py:106
  204.8 19.4 fusion.48
  284.8 37.8 %fusion.6 = (f32[3,8,1024]{2,1,0:T(8,128)S(1)}, f32[3,8,1024,1024]{3,2,1,0:T(8,128)}) fusion(pred[1024,1024]{0,1:T(8,128)(4,1)S(1)} %iota_compare_fusion, bf16[3,1024,8,96]{1,3,2,0:T(8,128)(2,1)} %all_to_all.101, bf16[3,1024,8,96]{1,3,2,0:T(8,128)(2,1)} %reshape.183), kind=kOutput, calls=%fused_computation.10 | convolution fusion | flops 4907311104 | bytes 111247360 | tf_op jit(solution)/shard_map/bqkge,bske->bkgqs/dot_general | solution.py:65
  322.7 31.2 fusion.5
  353.9 40.3 %convert_bitcast_fusion.3 = bf16[3,1024,8,96]{1,3,2,0:T(8,128)(2,1)} fusion(bf16[3,1024,8,96]{1,3,2,0:T(8,128)(2,1)} %all_to_all.97, f32[3,8,1024]{2,1,0:T(8,128)S(1)} %fusion.5, f32[3,8,1024]{2,1,0:T(8,128)S(1)} %get-tuple-element.24, f32[3,8,1024,1024]{3,2,1,0:T(8,128)} %get-tuple-element.25, pred[1024,1024]{0,1:T(8,128)(4,1)S(1)} %iota_compare_fusion), kind=kOutput, calls=%fused_computation.74 | convolution fusion | flops 4960026624 | bytes 111345664 | tf_op jit(solution)/shard_map/bkgqs,bske->bqkge/dot_general | solution.py:72
  425.4 78.4 %fusion = (f32[3,8,1024]{2,1,0:T(8,128)}, f32[3,8,1024,1024]{3,2,1,0:T(8,128)}) fusion(f32[3,8,1024]{2,1,0:T(8,128)S(1)} %fusion.5, f32[3,8,1024]{2,1,0:T(8,128)S(1)} %get-tuple-element.24, f32[3,8,1024,1024]{3,2,1,0:T(8,128)} %get-tuple-element.25, pred[1024,1024]{0,1:T(8,128)(4,1)S(1)} %iota_compare_fusion, bf16[3,1024,8,96]{1,3,2,0:T(8,128)(2,1)} %all_to_all.97, ...), kind=kOutput, calls=%fused_computation.3 | convolution fusion | flops 4982808576 | bytes 212107264 | tf_op jit(solution)/shard_map/bqkge,bske->bkgqs/dot_general | solution.py:79
  503.9 40.4 %convert_bitcast_fusion = bf16[3,1024,8,96]{1,3,2,0:T(8,128)(2,1)} fusion(bf16[3,1024,8,96]{1,3,2,0:T(8,128)(2,1)} %reshape.186, f32[3,8,1024]{2,1,0:T(8,128)S(1)} %fusion.5, f32[3,8,1024]{2,1,0:T(8,128)S(1)} %get-tuple-element.24, f32[3,8,1024,1024]{3,2,1,0:T(8,128)} %get-tuple-element.25, pred[1024,1024]{0,1:T(8,128)(4,1)S(1)} %iota_compare_fusion), kind=kOutput, calls=%fused_computation.71 | convolution fusion | flops 4960026624 | bytes 111345664 | tf_op jit(solution)/shard_map/bkgqs,bqkge->bske/dot_general | solution.py:78
  566.3 22.9 convolution_bitcast_fusion.1
  590.0 79.0 %fusion.11 = bf16[3,8,1024,1024]{2,3,1,0:T(8,128)(2,1)} fusion(f32[3,8,1024,1024]{3,2,1,0:T(8,128)} %get-tuple-element.27, f32[3,8,1024]{2,1,0:T(8,128)S(1)} %copy-done.5, f32[3,8,1024]{2,1,0:T(8,128)S(1)} %fusion.5, f32[3,8,1024]{2,1,0:T(8,128)S(1)} %get-tuple-element.24, f32[3,8,1024,1024]{3,2,1,0:T(8,128)} %get-tuple-element.25, ...), kind=kLoop, calls=%fused_computation.16 | loop fusion | flops 201326592 | bytes 253001728 | tf_op jit(solution)/shard_map/reshape.21
  669.0 21.4 convert_bitcast_fusion.2
  704.0 24.5 convert_bitcast_fusion.1
  736.9 105.3 %all-to-all-done.5 = bf16[3,1024,8,96]{3,2,0,1:T(8,128)(2,1)} async-done(((bf16[3,1024,8,96]{3,2,0,1:T(8,128)(2,1)}), bf16[3,1024,8,96]{3,2,0,1:T(8,128)(2,1)}, u32[]{:S(2)}, u32[]{:S(2)}) %all-to-all-start.5) | async-done | bytes 4718624 | tf_op jit(solution)/shard_map/all_to_all | solution.py:117
  876.7 108.9 %all-to-all-done.6 = bf16[3,1024,8,96]{3,2,0,1:T(8,128)(2,1)} async-done(((bf16[3,1024,8,96]{3,2,0,1:T(8,128)(2,1)}), bf16[3,1024,8,96]{3,2,0,1:T(8,128)(2,1)}, u32[]{:S(2)}, u32[]{:S(2)}) %all-to-all-start.6) | async-done | bytes 4718624 | tf_op jit(solution)/shard_map/all_to_all | solution.py:118
  1016.8 62.8 %convolution_bitcast_fusion = f32[3072,9216]{1,0:T(8,128)} fusion(bf16[3,256,3072]{2,1,0:T(8,128)(2,1)} %copy.97, bf16[3,256,3072]{2,1,0:T(8,128)(2,1)} %copy.96, bf16[3,256,3072]{2,1,0:T(8,128)(2,1)} %copy.95, bf16[3,256,3072]{2,1,0:T(8,128)(2,1)} %param.6, f32[3072]{0:T(1024)S(1)} %copy-done.7, f32[3,256]{1,0:T(4,128)S(1)} %copy-done.9), kind=kOutput, calls=%fused_computation.11 | convolution fusion | flops 43538448384 | bytes 132135936 | tf_op jit(solution)/shard_map/btd,btw->dw/dot_general | solution.py:119
  1079.6 57.9 %fusion.31 = (f32[3072]{0:T(1024)S(1)}, f32[3,256]{1,0:T(4,128)S(1)}, f32[3,256,3072]{2,1,0:T(8,128)}) fusion(bf16[3,256,3072]{2,1,0:T(8,128)(2,1)} %param.6, f32[3,256]{1,0:T(4,128)S(1)} %copy-done.9, f32[3072]{0:T(1024)S(1)} %copy-done.7, bf16[3072,9216]{1,0:T(8,128)(2,1)} %param.8, bf16[3,256,3072]{2,1,0:T(8,128)(2,1)} %copy.97, ...), kind=kOutput, calls=%fused_computation.41 | convolution fusion | flops 43545522176 | bytes 84965376 | tf_op jit(solution)/shard_map/btw,dw->btd/dot_general | solution.py:120
  1137.5 12.1 psum.23
  1149.6 11.3 fusion.30
  1164.5 18.1 fusion.33
  1182.6 197.7 %all-reduce.5.cloned.1.call-done = f32[32,96,3072]{2,1,0:T(8,128)} async-done(((f32[32,96,3072]{2,1,0:T(8,128)}), f32[32,96,3072]{2,1,0:T(8,128)}) %all-reduce.5.cloned.1.call-update) | async-done | bytes 37748752 | tf_op jit(solution)/shard_map/psum | solution.py:123
  1380.2 1838.5 %all-reduce.3.cloned.1.call-done = f32[3072,9216]{1,0:T(8,128)} async-done(((f32[3072,9216]{1,0:T(8,128)}), f32[3072,9216]{1,0:T(8,128)}) %all-reduce.3.cloned.1.call-update) | async-done | bytes 113246224 | tf_op jit(solution)/shard_map/psum | solution.py:123
  3218.7 74.3 %copy.117 = f32[3072,9216]{1,0:T(8,128)} copy(f32[3072,9216]{1,0:T(8,128)} %all-reduce.3.cloned.1.call-done) | data formatting | bytes 226492416
  3293.0 28.1 copy.118
  (80 shorter events, 289.4 us)
Async XLA Ops:
  7.9 55.8 %copy-start.6 = (f32[3072]{0:T(1024)}, f32[3072]{0:T(1024)S(1)}, u32[]{:S(2)}) copy-start(f32[3072]{0:T(1024)S(1)} %convert_element_type.102) | copy-start | bytes 36868
  11.2 52.5 %copy-start.8 = (f32[3,256]{1,0:T(4,128)}, f32[3,256]{1,0:T(4,128)S(1)}, u32[]{:S(2)}) copy-start(f32[3,256]{1,0:T(4,128)S(1)} %add_rsqrt_fusion) | copy-start | bytes 9220
  81.7 59.5 %all-to-all-start = ((bf16[3,256,32,96]{1,3,0,2:T(8,128)(2,1)}), bf16[3,256,32,96]{1,3,0,2:T(8,128)(2,1)}, u32[]{:S(2)}, u32[]{:S(2)}) async-start(bf16[3,256,32,96]{1,3,0,2:T(8,128)(2,1)} %copy.72), calls=%async_computation | async-start | bytes 9437184 | tf_op jit(solution)/shard_map/all_to_all | solution.py:107
  109.0 9.6 copy-start.10
  119.5 9.3 copy-start.2
  141.2 58.4 %all-to-all-start.1 = ((bf16[3,256,32,96]{1,3,0,2:T(8,128)(2,1)}), bf16[3,256,32,96]{1,3,0,2:T(8,128)(2,1)}, u32[]{:S(2)}, u32[]{:S(2)}) async-start(bf16[3,256,32,96]{1,3,0,2:T(8,128)(2,1)} %copy.75), calls=%async_computation.1 | async-start | bytes 9437184 | tf_op jit(solution)/shard_map/all_to_all | solution.py:106
  199.6 62.8 %all-to-all-start.2 = ((bf16[3,256,32,96]{1,3,0,2:T(8,128)(2,1)}), bf16[3,256,32,96]{1,3,0,2:T(8,128)(2,1)}, u32[]{:S(2)}, u32[]{:S(2)}) async-start(bf16[3,256,32,96]{1,3,0,2:T(8,128)(2,1)} %copy.78), calls=%async_computation.2 | async-start | bytes 9437184 | tf_op jit(solution)/shard_map/all_to_all | solution.py:105
  262.4 140.1 %all-to-all-start.4 = ((bf16[3,256,32,96]{1,3,0,2:T(8,128)(2,1)}), bf16[3,256,32,96]{1,3,0,2:T(8,128)(2,1)}, u32[]{:S(2)}, u32[]{:S(2)}) async-start(bf16[3,256,32,96]{1,3,0,2:T(8,128)(2,1)} %copy.83), calls=%async_computation.4 | async-start | bytes 9437184 | tf_op jit(solution)/shard_map/all_to_all | solution.py:115
  402.5 150.0 %all-to-all-start.3 = ((bf16[3,1024,8,96]{3,2,0,1:T(8,128)(2,1)}), bf16[3,1024,8,96]{3,2,0,1:T(8,128)(2,1)}, u32[]{:S(2)}, u32[]{:S(2)}) async-start(bf16[3,1024,8,96]{3,2,0,1:T(8,128)(2,1)} %copy.81), calls=%async_computation.3 | async-start | bytes 12582912 | tf_op jit(solution)/shard_map/all_to_all | solution.py:109
  552.6 146.2 %all-to-all-start.7 = ((bf16[3,1024,8,96]{3,2,0,1:T(8,128)(2,1)}), bf16[3,1024,8,96]{3,2,0,1:T(8,128)(2,1)}, u32[]{:S(2)}, u32[]{:S(2)}) async-start(bf16[3,1024,8,96]{3,2,0,1:T(8,128)(2,1)} %copy.92), calls=%async_computation.7 | async-start | bytes 12582912 | tf_op jit(solution)/shard_map/all_to_all | solution.py:118
  557.8 822.4 %all-reduce.5.cloned.1.call-start = ((), (), s32[]{:S(2)}) async-start(), calls=%async_computation.9 | async-start | bytes 75497472 | tf_op jit(solution)/shard_map/psum | solution.py:123
  589.1 0.9 copy-start.5
  698.7 143.5 %all-to-all-start.5 = ((bf16[3,1024,8,96]{3,2,0,1:T(8,128)(2,1)}), bf16[3,1024,8,96]{3,2,0,1:T(8,128)(2,1)}, u32[]{:S(2)}, u32[]{:S(2)}) async-start(bf16[3,1024,8,96]{3,2,0,1:T(8,128)(2,1)} %copy.86), calls=%async_computation.5 | async-start | bytes 12582912 | tf_op jit(solution)/shard_map/all_to_all | solution.py:117
  842.2 143.4 %all-to-all-start.6 = ((bf16[3,1024,8,96]{3,2,0,1:T(8,128)(2,1)}), bf16[3,1024,8,96]{3,2,0,1:T(8,128)(2,1)}, u32[]{:S(2)}, u32[]{:S(2)}) async-start(bf16[3,1024,8,96]{3,2,0,1:T(8,128)(2,1)} %copy.89), calls=%async_computation.6 | async-start | bytes 12582912 | tf_op jit(solution)/shard_map/all_to_all | solution.py:118
  847.4 2371.3 %all-reduce.3.cloned.1.call-start = ((), (), s32[]{:S(2)}) async-start(), calls=%async_computation.8 | async-start | bytes 226492416 | tf_op jit(solution)/shard_map/psum | solution.py:123
  876.7 117.3 %copy-start.3 = (f32[256,48]{0,1:T(8,128)S(1)}, f32[256,48]{0,1:T(8,128)}, u32[]{:S(2)}) copy-start(f32[256,48]{0,1:T(8,128)} %copy-done.2) | copy-start | bytes 147460
  876.7 117.3 %copy-start.4 = (f32[256,48]{0,1:T(8,128)S(1)}, f32[256,48]{0,1:T(8,128)}, u32[]{:S(2)}) copy-start(f32[256,48]{0,1:T(8,128)} %get-tuple-element.21) | copy-start | bytes 147460
  1010.1 6.7 copy-start.7
  1010.1 6.7 copy-start.9
  1149.6 13.5 copy-start
  1149.6 14.9 copy-start.1
Sparse Core Ops, SparseCore 0:
  589.3 790.8 all-reduce.4
  1383.3 1835.3 all-reduce.2
where the time goes:
time: 3340 us; the launch traced here: 3330 us
  waiting for transfers between devices  2310 us (69%)
  matrix products  476 us (14%)
  local copies, waits for them, and re-layouts  327 us (10%)
  other arithmetic  148 us (4%)
  starting transfers between devices  41.3 us (1%)
    psum x1, waiting for transfers between devices, device_step(): lax.psum(grad_w_qkv, 'sp')  1840 us
    psum x1, waiting for transfers between devices, device_step(): lax.psum(grad_w_out, 'sp')  198 us
    all_to_all x1, waiting for transfers between devices, device_step(): to_tokens(grad_k)  109 us
    unnamed x24, local copies, waits for them, and re-layouts  107 us
    all_to_all x1, waiting for transfers between devices, device_step(): to_tokens(grad_q.reshape(n_batch, seq_len, heads_local, head_dim))  105 us
    another operation x3, other arithmetic  93.7 us
    dot_general x1, matrix products, attention_backward(): jnp.einsum('bqkge,bske->bkgqs', grad_attn, value_vals, preferred_element_...  78.4 us
  transfers between devices with their start and end apart: 10, of which 6 were waited for; matrix products, arithmetic and copies ran while one was open for 23% of the time, Pallas kernels for 0%

commit v1 on v0

v1 whole, which is shorter than its diff:
```python
import functools
import math

import jax
import jax.numpy as jnp
from jax import lax
from jax.experimental import pallas as pl
from jax.experimental.pallas import tpu as pltpu
from jax.sharding import PartitionSpec as P


NORM_EPS = 1e-5
ROPE_BASE = 10000.0
ROPE_GAIN = math.sqrt(1.0 + math.log(32.0) / math.log(4096.0))
MASK_VALUE = -1e30
LOG2E = math.log2(math.e)
LANES = 128
CHUNK_NN, CHUNK_NT = 128, 256
VMEM_LIMIT = 60 * 1024 * 1024

ANY = pl.BlockSpec(memory_space=pl.ANY)


def params(sems):
    return pltpu.CompilerParams(dimension_semantics=sems, vmem_limit_bytes=VMEM_LIMIT)


def cost(flops, bytes_accessed, transcendentals=0):
    return pl.CostEstimate(flops=flops, bytes_accessed=bytes_accessed, transcendentals=transcendentals)


def rope_tables(seq_len, long_factor, head_dim):
    half_rot = long_factor.shape[0]
    exponent = jnp.arange(half_rot, dtype=jnp.float32) / half_rot
    inv_freq = 1.0 / (long_factor * jnp.power(ROPE_BASE, exponent))
    angles = jnp.arange(seq_len, dtype=jnp.float32)[:, None] * inv_freq[None, :]
    cos_t, sin_t = jnp.cos(angles) * ROPE_GAIN, jnp.sin(angles) * ROPE_GAIN
    pad = jnp.zeros((seq_len, LANES - head_dim), jnp.float32)
    return jnp.concatenate([cos_t, cos_t, pad], axis=1), jnp.concatenate([-sin_t, sin_t, pad], axis=1)


def lane_iota(rows):
    return lax.broadcasted_iota(jnp.int32, (rows, LANES), 1)


def swap_halves(vals, lane, half):
    return jnp.where(lane < half, pltpu.roll(vals, LANES - half, 1), pltpu.roll(vals, half, 1))


def head_of(acc, index, head_dim, lane):
    tile, off = divmod(index * head_dim, LANES)
    low = acc[:, tile * LANES:(tile + 1) * LANES]
    if off == 0:
        return low
    if off + head_dim > LANES:
        low = jnp.where(lane >= off, low, acc[:, (tile + 1) * LANES:(tile + 2) * LANES])
    return pltpu.roll(low, LANES - off, 1)


def pack_heads(heads, head_dim, lane):
    rolled = [heads[0]] + [pltpu.roll(h, LANES - (LANES - i * head_dim % LANES) % LANES, 1) for i, h in enumerate(heads) if i]
    n_tiles = len(heads) * head_dim // LANES
    return [jnp.where(lane < (t + 1) * head_dim - t * LANES, rolled[t], rolled[t + 1]) for t in range(n_tiles)]


def proj_kernel(rope, heads_blk, head_dim, me_ref, x0, x1, w, *rest):
    if rope:
        cos_ref, sin_ref, _, _, out, x_all = rest
    else:
        _, _, out, x_all = rest
    core = lax.rem(me_ref[0], 2)
    rows = CHUNK_NN if rope else CHUNK_NT
    lane = lane_iota(rows)
    col = pl.program_id(1)
    contract = (((1,), (0,)), ((), ())) if rope else (((1,), (1,)), ((), ()))

    @pl.when(col == 0)
    def _():
        x_all[0, core] = x0[0]
        x_all[0, 1 - core] = x1[0]

    ones = jnp.where(lane < head_dim, 1.0, 0.0)
    for x, place, off in [(x, place, off) for x, place in ((x0, core), (x1, 1 - core)) for off in range(0, x0.shape[1], rows)]:
        start = pl.multiple_of(place * x0.shape[1] + off, rows)
        acc = lax.dot_general(x[0, off:off + rows, :], w[...], contract, preferred_element_type=jnp.float32)
        if rope:
            plain = col >= 4
            cos_t = jnp.where(plain, ones, cos_ref[pl.ds(start, rows), :])
            sin_t = jnp.where(plain, 0.0, sin_ref[pl.ds(start, rows), :])
        for h in range(heads_blk):
            vals = head_of(acc, h, head_dim, lane)
            if rope:
                vals = vals * cos_t + swap_halves(vals, lane, head_dim // 2) * sin_t
                out[0, h, pl.ds(start, rows), :] = vals.astype(jnp.bfloat16)
            else:
                out[h, pl.ds(start, rows), :] = jnp.where(lane < head_dim, vals, 0.0).astype(jnp.bfloat16)


def project(me, x0, x1, batch0, other, w, tables, bufs, n_batch, head_dim, heads_mine):
    nb, rows, d = x0.shape
    rope = tables is not None
    heads_blk = 8
    wid = heads_blk * head_dim
    blocks = heads_mine // heads_blk
    cols = 3 * blocks if rope else blocks

    def pair(me_ref):
        own = me_ref[0] // 2
        return 1 - own if other else own

    x_spec = pl.BlockSpec((1, rows, d), lambda i, j, m: (i, 0, 0))
    if rope:
        w_spec = pl.BlockSpec((d, wid), lambda i, j, m: (0, (j // blocks) * 2 * blocks + lax.rem(m[0], 2) * blocks + lax.rem(j, blocks)))
        t_spec = pl.BlockSpec((2 * rows, LANES), lambda i, j, m: (pair(m), 0))
        o_spec = pl.BlockSpec((1, heads_blk, 2 * rows, LANES), lambda i, j, m: (j // blocks, lax.rem(j, blocks), (i + batch0) * 2 + pair(m), 0))
        o_shape = jax.ShapeDtypeStruct((3, heads_mine, n_batch * 4 * rows, LANES), jnp.bfloat16)
        extra, extra_specs = list(tables), [t_spec, t_spec]
    else:
        w_spec = pl.BlockSpec((wid, d), lambda i, j, m: (lax.rem(m[0], 2) * blocks + j, 0))
        o_spec = pl.BlockSpec((heads_blk, 2 * rows, LANES), lambda i, j, m: (j, (i + batch0) * 2 + pair(m), 0))
        o_shape = jax.ShapeDtypeStruct((heads_mine, n_batch * 4 * rows, LANES), jnp.bfloat16)
        extra, extra_specs = [], []
    a_spec = pl.BlockSpec((1, 2, rows, d), lambda i, j, m: (i + batch0, pair(m), 0, 0))
    a_shape = jax.ShapeDtypeStruct((n_batch, 4, rows, d), jnp.bfloat16)
    first = bufs is None
    if first:
        bufs = (jnp.zeros((8, LANES), jnp.bfloat16),) * 2
    n_in = 4 + len(extra)
    return pl.pallas_call(
        functools.partial(proj_kernel, rope, heads_blk, head_dim),
        grid_spec=pltpu.PrefetchScalarGridSpec(
            num_scalar_prefetch=1, grid=(nb, cols),
            in_specs=[x_spec, x_spec, w_spec] + extra_specs + [ANY, ANY],
            out_specs=[o_spec, a_spec]),
        out_shape=[o_shape, a_shape],
        input_output_aliases={} if first else {n_in: 0, n_in + 1: 1},
        compiler_params=params(("arbitrary", "arbitrary")),
        cost_estimate=cost(2 * nb * 2 * rows * d * wid * cols, nb * (cols * d * wid * 2 + 8 * rows * d)),
        name="project_qkv" if rope else "project_grad",
    )(me, x0, x1, w, *extra, *bufs)


def attn_kernel(head_dim, q, k, v, g, cos_ref, sin_ref, *rest):
    o_out, d_out, acc_o, acc_q, acc_k, acc_v = rest[-6:]
    n_heads, seq = q.shape[1], q.shape[2]
    blk = 256
    per_step = 1
    nblk = seq // blk
    scale = head_dim ** -0.5
    row = lax.broadcasted_iota(jnp.int32, (blk, blk), 0)
    column = lax.broadcasted_iota(jnp.int32, (blk, blk), 1)
    causal = row >= column
    dot = functools.partial(lax.dot_general, preferred_element_type=jnp.float32)
    nt = (((1,), (1,)), ((), ()))
    nn = (((1,), (0,)), ((), ()))
    tn = (((0,), (0,)), ((), ()))

    def some_heads(step, carry):
        for p in range(nblk):
            for h in [step * per_step + n for n in range(per_step)]:
                rows = slice(p * blk, (p + 1) * blk)
                keys = (p + 1) * blk
                qp, gp = q[0, h, rows, :], g[h, rows, :]
                kc, vc = k[0, h, :keys, :], v[0, h, :keys, :]
                s = dot(qp, kc, nt)
                diag = jnp.where(causal, s[:, p * blk:], MASK_VALUE)
                s = diag if p == 0 else jnp.concatenate([s[:, :p * blk], diag], axis=1)
                top = jnp.max(s, axis=1, keepdims=True)
                e = jnp.exp2((s - top) * (scale * LOG2E))
                prob = e * (1.0 / jnp.sum(e, axis=1, keepdims=True))
                pb = prob.astype(jnp.bfloat16)
                o = dot(pb, vc, nn)
                row_dot = jnp.sum(gp.astype(jnp.float32) * o, axis=1, keepdims=True)
                dp = dot(gp, vc, nt)
                ds = (prob * (dp - row_dot)).astype(jnp.bfloat16)
                acc_o[h, rows, :] = o
                acc_q[h, rows, :] = dot(ds, kc, nn) * scale
                dk = dot(ds, qp, tn)
                dv = dot(pb, gp, tn)
                if p:
                    acc_k[h, :p * blk, :] += dk[:p * blk]
                    acc_v[h, :p * blk, :] += dv[:p * blk]
                acc_k[h, rows, :] = dk[p * blk:]
                acc_v[h, rows, :] = dv[p * blk:]
        return carry

    lax.fori_loop(0, n_heads // per_step, some_heads, 0)

    lane = lane_iota(blk)

    def store(p, carry):
        rows = pl.ds(pl.multiple_of(p * blk, blk), blk)
        cos_t, sin_t = cos_ref[rows, :], sin_ref[rows, :]
        for which, acc in enumerate((acc_q, acc_k, acc_v, acc_o)):
            heads = []
            for h in range(n_heads):
                vals = acc[h, rows, :]
                if which == 1:
                    vals = vals * scale
                if which < 2:
                    vals = vals * cos_t - swap_halves(vals, lane, head_dim // 2) * sin_t
                heads.append(vals)
            tiles = pack_heads(heads, head_dim, lane)
            for t, vals in enumerate(tiles):
                vals = vals.astype(jnp.bfloat16)
                if which == 3:
                    o_out[0, rows, t * LANES:(t + 1) * LANES] = vals
                else:
                    d_out[which, 0, rows, t * LANES:(t + 1) * LANES] = vals
        return carry

    lax.fori_loop(0, nblk, store, 0)


def attention(qkv, grad_heads, tables, batch, bufs, n_batch, seq, head_dim):
    heads_mine = qkv.shape[1]
    group = 4
    wid = group * head_dim
    in_spec = lambda part: pl.BlockSpec((1, group, seq, LANES), lambda i, part=part: (part, i, batch, 0))
    g_spec = pl.BlockSpec((group, seq, LANES), lambda i: (i, batch, 0))
    t_spec = pl.BlockSpec((seq, LANES), lambda i: (0, 0))
    first = bufs is None
    bufs = [] if first else list(bufs)
    return pl.pallas_call(
        functools.partial(attn_kernel, head_dim),
        grid=(heads_mine // group,),
        in_specs=[in_spec(0), in_spec(1), in_spec(2), g_spec, t_spec, t_spec] + [ANY] * len(bufs),
        out_specs=[pl.BlockSpec((1, seq, wid), lambda i: (batch, 0, i)),
                   pl.BlockSpec((3, 1, seq, wid), lambda i: (0, batch, 0, i))],
        out_shape=[jax.ShapeDtypeStruct((n_batch, seq, heads_mine * head_dim), jnp.bfloat16),
                   jax.ShapeDtypeStruct((3, n_batch, seq, heads_mine * head_dim), jnp.bfloat16)],
        scratch_shapes=[pltpu.VMEM((group, seq, LANES), jnp.float32)] * 4,
        input_output_aliases={} if first else {6: 0, 7: 1},
        compiler_params=params(("arbitrary",)),
        cost_estimate=cost(heads_mine * 6 * 2 * seq * seq * 256 * 5 // 8, heads_mine * seq * 128 * 2 * 8, heads_mine * seq * seq),
        name="attention",
    )(qkv, qkv, qkv, grad_heads, *tables, *bufs)


def wgrad_kernel(me_ref, lhs, rhs, *rest):
    full, mine = rest[-2:]
    vals = lax.dot_general(lhs[...], rhs[...], (((0,), (0,)), ((), ())), preferred_element_type=jnp.float32)
    full[...] = vals
    mine[...] = vals


def weight_grad(me, lhs, rhs, full_shape, place, buf, part=None, blk_r=512, blk_c=768):
    tok, n_r = lhs.shape
    n_c = rhs.shape[-1]
    rhs_spec = pl.BlockSpec((tok, blk_c), lambda j, i, m: (0, j)) if part is None else pl.BlockSpec((None, tok, blk_c), lambda j, i, m: (part, 0, j))
    first = buf is None
    bufs = [] if first else [buf]
    return pl.pallas_call(
        wgrad_kernel,
        grid_spec=pltpu.PrefetchScalarGridSpec(
            num_scalar_prefetch=1, grid=(n_c // blk_c, n_r // blk_r),
            in_specs=[pl.BlockSpec((tok, blk_r), lambda j, i, m: (0, i)), rhs_spec] + [ANY] * len(bufs),
            out_specs=[pl.BlockSpec((blk_r, blk_c), lambda j, i, m: place(i, j, lax.rem(m[0], 2))),
                       pl.BlockSpec((blk_r, blk_c), lambda j, i, m: (i, j))]),
        out_shape=[jax.ShapeDtypeStruct(full_shape, jnp.float32), jax.ShapeDtypeStruct((n_r, n_c), jnp.float32)],
        input_output_aliases={} if first else {3: 0},
        compiler_params=params(("arbitrary", "arbitrary")),
        cost_estimate=cost(2 * tok * n_r * n_c, 2 * tok * (n_r * (n_c // blk_c) + n_c) + 8 * n_r * n_c),
        name="weight_grad",
    )(me, lhs, rhs, *bufs)


def place_kernel(me_ref, part, _, full):
    full[...] = part[...]


def place_part(me, part, full, place, blk_r=512, blk_c=1536):
    n_r, n_c = part.shape
    return pl.pallas_call(
        place_kernel,
        grid_spec=pltpu.PrefetchScalarGridSpec(
            num_scalar_prefetch=1, grid=(n_c // blk_c, n_r // blk_r),
            in_specs=[pl.BlockSpec((blk_r, blk_c), lambda j, i, m: (i, j)), ANY],
            out_specs=pl.BlockSpec((blk_r, blk_c), lambda j, i, m: place(i, j, 1 - lax.rem(m[0], 2)))),
        out_shape=jax.ShapeDtypeStruct(full.shape, jnp.float32),
        input_output_aliases={2: 0},
        compiler_params=params(("arbitrary", "arbitrary")),
        cost_estimate=cost(n_r * n_c * 40, 8 * n_r * n_c),
        name="place_part",
    )(me, part, full)


def solution(mesh):
    core_perm = [(0, 1), (1, 0), (2, 3), (3, 2)]
    chip_perm = [(0, 2), (1, 3), (2, 0), (3, 1)]
    to_core = functools.partial(lax.ppermute, axis_name='sp', perm=core_perm)
    to_chip = functools.partial(lax.ppermute, axis_name='sp', perm=chip_perm)

    def device_step(hidden, norm_w, w_qkv, w_out, long_factor, grad_out):
        n_batch, tok, d = hidden.shape
        n_heads, head_dim = w_out.shape[0], w_out.shape[1]
        heads_mine = n_heads // 2
        wid = heads_mine * head_dim
        seq = 4 * tok
        index = lax.axis_index('sp')
        me = jnp.reshape(index, (1,)).astype(jnp.int32)
        core = lax.rem(index, 2)
        partner = index + 1 - 2 * core
        w_out2 = w_out.reshape(n_heads * head_dim, d)
        tables = rope_tables(seq, long_factor, head_dim)
        gain = norm_w.astype(jnp.float32)

        hidden_f = hidden.astype(jnp.float32)
        inv_rms = lax.rsqrt(jnp.mean(hidden_f * hidden_f, axis=-1, keepdims=True) + NORM_EPS)
        normed = (hidden_f * inv_rms * gain).astype(jnp.bfloat16)

        near_n, near_g = to_core(normed), to_core(grad_out)
        far_n = [to_chip(normed[b:b + 1]) for b in range(n_batch)]
        far_g = [to_chip(grad_out[b:b + 1]) for b in range(n_batch)]

        proj = functools.partial(project, me, n_batch=n_batch, head_dim=head_dim, heads_mine=heads_mine)
        qkv = proj(normed, near_n, 0, False, w_qkv, tables, None)
        grd = proj(grad_out, near_g, 0, False, w_out2, None, None)
        relay_n = [to_core(f) for f in far_n]
        relay_g = [to_core(f) for f in far_g]
        att = None
        for b in range(n_batch):
            qkv = proj(far_n[b], relay_n[b], b, True, w_qkv, tables, qkv)
        for b in range(n_batch):
            grd = proj(far_g[b], relay_g[b], b, True, w_out2, None, grd)
            att = attention(qkv[0], grd[0], tables, b, att, n_batch, seq, head_dim)
        attn, grad_fused = att
        normed_all = qkv[1].reshape(n_batch * seq, d)
        grad_out_all = grd[1].reshape(n_batch * seq, d)

        def own_tokens(vals, axis):
            mine = lax.dynamic_slice_in_dim(vals, index * tok, tok, axis)
            theirs = lax.dynamic_slice_in_dim(vals, partner * tok, tok, axis)
            return mine, to_core(theirs)

        a_mine, a_recv = own_tokens(attn, 1)
        f_mine, f_recv = own_tokens(grad_fused, 2)

        place_o = lambda i, j, c: (c * (wid // 512) + i, j)
        g_wo, mine_wo = weight_grad(me, attn.reshape(n_batch * seq, wid), grad_out_all, (2 * wid, d), place_o, None)
        recv_wo = to_core(mine_wo)

        even = core == 0
        attn_local = jnp.concatenate([jnp.where(even, a_mine, a_recv), jnp.where(even, a_recv, a_mine)], axis=-1)
        projected = jnp.einsum('btw,wd->btd', attn_local, w_out2, preferred_element_type=jnp.float32)
        block_out = (hidden_f + projected).astype(jnp.bfloat16)

        g_wqkv, recv = None, []
        fused_tok = grad_fused.reshape(3, n_batch * seq, wid)
        for part in range(3):
            place_p = lambda i, j, c, part=part: (i, part * 4 + c * 2 + j)
            g_wqkv, mine = weight_grad(me, normed_all, fused_tok, (d, 6 * wid), place_p, g_wqkv, part)
            recv.append(to_core(mine))

        pieces = []
        for part in range(3):
            pieces += [jnp.where(even, f_mine[part], f_recv[part]), jnp.where(even, f_recv[part], f_mine[part])]
        fused_local = jnp.concatenate(pieces, axis=-1)
        grad_normed = jnp.einsum('btw,dw->btd', fused_local, w_qkv, preferred_element_type=jnp.float32)
        unit_rows = hidden_f * inv_rms
        grad_unit = grad_normed * gain
        mean_dot = jnp.mean(grad_unit * unit_rows, axis=-1, keepdims=True)
        grad_hidden = (grad_out.astype(jnp.float32) + inv_rms * (grad_unit - unit_rows * mean_dot)).astype(jnp.bfloat16)
        g_norm = jnp.sum(grad_normed * unit_rows, axis=(0, 1))
        g_norm = g_norm + to_core(g_norm)
        g_norm = g_norm + to_chip(g_norm)

        g_wo = place_part(me, recv_wo, g_wo, lambda i, j, c: (c * (wid // 512) + i, j))
        for part in range(3):
            g_wqkv = place_part(me, recv[part], g_wqkv, lambda i, j, c, part=part: (i, part * 2 + c))
        return (block_out, grad_hidden, g_wqkv, g_wo.reshape(n_heads, head_dim, d), g_norm)

    tok_spec = P('dp', 'sp', None)

    return jax.shard_map(device_step, mesh=mesh,
                         in_specs=(tok_spec, P(), P(), P(), P(), tok_spec),
                         out_specs=(tok_spec, tok_spec, P('dp', None), P('dp', None, None), P('dp')),
                         check_vma=False)
```

time: 3340 us -> 939 us (0.28)
  waiting for transfers between devices: 2310 us -> 99.9 us
  Pallas kernels: 0 us -> 665 us
  matrix products: 476 us -> 74.6 us
  local copies, waits for them, and re-layouts: 327 us -> 19.7 us
  other arithmetic: 148 us -> 55.1 us
    psum x2 -> x0, waiting for transfers between devices: 2040 us -> none  [the longest x1 1840 us: device_step(): lax.psum(grad_w_qkv, 'sp')]
    pallas_call x0 -> x19, Pallas kernels: none -> 665 us  [the longest x3 247 us: attention(): pl.pallas_call(functools.partial(attn_kernel, head_dim), grid=(heads_mine...]
    dot_general x12 -> x2, matrix products: 476 us -> 74.6 us  [the longest x1 55.4 us: device_step(): jnp.einsum('btw,dw->btd', fused_local, w_qkv, preferred_element_type=jnp....]
    all_to_all x8 -> x0, waiting for transfers between devices: 272 us -> none  [the longest x1 109 us: device_step(): to_tokens(grad_k)]
    unnamed x24 -> x18, local copies, waits for them, and re-layouts: 107 us -> 0.19 us
    ppermute x0 -> x22, waiting for transfers between devices: none -> 99.9 us  [the longest x3 88.8 us: device_step(): far_n = [to_chip(normed[b:b + 1]) for b in range(n_batch)]]
    another operation x3 -> x0, other arithmetic: 93.7 us -> none
    all_to_all x9 -> x0, local copies, waits for them, and re-layouts: 78.1 us -> none  [the longest x2 17.9 us: device_step(): v_heads = to_heads(v_local)]
  transfers between devices with their start and end apart: 10 -> 22, of which waited for: 6 -> 5; matrix products, arithmetic and copies ran while one was open for 23% -> 15% of each run, Pallas kernels for 0% -> 60%
where the time goes in v1:
time: 939 us; the launch traced here: 932 us
  Pallas kernels  665 us (71%)
  waiting for transfers between devices  99.9 us (11%)
  matrix products  74.6 us (8%)
  other arithmetic  55.1 us (6%)
  local copies, waits for them, and re-layouts  19.7 us (2%)
  starting transfers between devices  16.5 us (2%)
    pallas_call x3, Pallas kernels, attention(): pl.pallas_call(functools.partial(attn_kernel, head_dim), grid=(heads_mine...  247 us
    pallas_call x8, Pallas kernels, project(): pl.pallas_call(functools.partial(proj_kernel, rope, heads_blk, head_dim),...  192 us
    pallas_call x4, Pallas kernels, weight_grad(): pl.pallas_call(wgrad_kernel, grid_spec=pltpu.PrefetchScalarGridSpec(num_s...  171 us
    ppermute x3, waiting for transfers between devices, device_step(): far_n = [to_chip(normed[b:b + 1]) for b in range(n_batch)]  88.8 us
    dot_general x1, matrix products, device_step(): jnp.einsum('btw,dw->btd', fused_local, w_qkv, preferred_element_type=jnp....  55.4 us
    pallas_call x4, Pallas kernels, place_part(): pl.pallas_call(place_kernel, grid_spec=pltpu.PrefetchScalarGridSpec(num_s...  55.3 us
    unnamed x6, other arithmetic  22.4 us
    dot_general x1, matrix products, device_step(): jnp.einsum('btw,wd->btd', attn_local, w_out2, preferred_element_type=jnp....  19.3 us
  transfers between devices with their start and end apart: 22, of which 5 were waited for; matrix products, arithmetic and copies ran while one was open for 15% of the time, Pallas kernels for 60%

profile of v1, /device:TPU:0, one launch (start us, length us, event | category | flops | bytes accessed | tf_op | source)
XLA Modules:
  0.0 932.0 jit_solution(9196181615467499538)
XLA Ops:
  29.2 25.4 %collective-permute-done.x0 = bf16[1,256,3072]{2,1,0:T(8,128)(2,1)S(1)} collective-permute-done((bf16[1,256,3072]{2,1,0:T(8,128)(2,1)}, bf16[1,256,3072]{2,1,0:T(8,128)(2,1)S(1)}, u32[]{:S(2)}, u32[]{:S(2)}) %collective-permute-start) | collective-permute-done | bytes 1572896 | tf_op jit(solution)/shard_map/ppermute | solution.py:313
  56.6 31.7 %collective-permute-done.2.x0 = bf16[1,256,3072]{2,1,0:T(8,128)(2,1)S(1)} collective-permute-done((bf16[1,256,3072]{2,1,0:T(8,128)(2,1)}, bf16[1,256,3072]{2,1,0:T(8,128)(2,1)S(1)}, u32[]{:S(2)}, u32[]{:S(2)}) %collective-permute-start.2) | collective-permute-done | bytes 1572896 | tf_op jit(solution)/shard_map/ppermute | solution.py:313
  90.3 31.8 %collective-permute-done.4.x0 = bf16[1,256,3072]{2,1,0:T(8,128)(2,1)} collective-permute-done((bf16[1,256,3072]{2,1,0:T(8,128)(2,1)}, bf16[1,256,3072]{2,1,0:T(8,128)(2,1)}, u32[]{:S(2)}, u32[]{:S(2)}) %collective-permute-start.4) | collective-permute-done | bytes 1572896 | tf_op jit(solution)/shard_map/ppermute | solution.py:313
  124.7 62.6 %project_qkv.4 = (bf16[3,16,3072,128]{3,2,1,0:T(8,128)(2,1)}, bf16[3,4,256,3072]{3,2,1,0:T(8,128)(2,1)}) custom-call(s32[1]{0:T(128)} %bitcast.me_ref, bf16[3,256,3072]{2,1,0:T(8,128)(2,1)} %fusion.6.x0, bf16[3,256,3072]{2,1,0:T(8,128)(2,1)} %collective-permute-done.6.x1, bf16[3072,9216]{1,0:T(8,128)(2,1)} %w.7, ...), custom_call_target="tpu_custom_call" | custom-call | flops 43486543872 | bytes 103809024 | tf_op jit(solution)/shard_map/project_qkv/pallas_call | solution.py:129
  187.8 24.6 %project_grad.4 = (bf16[16,3072,128]{2,1,0:T(8,128)(2,1)}, bf16[3,4,256,3072]{3,2,1,0:T(8,128)(2,1)}) custom-call(s32[1]{0:T(128)} %bitcast.me_ref, bf16[3,256,3072]{2,1,0:T(8,128)(2,1)} %x0.1, bf16[3,256,3072]{2,1,0:T(8,128)(2,1)} %collective-permute-done.13.x1, bf16[3072,3072]{1,0:T(8,128)(2,1)} %bitcast.34, ...), custom_call_target="tpu_custom_call" | custom-call | flops 14495514624 | bytes 47185920 | tf_op jit(solution)/shard_map/project_grad/pallas_call | solution.py:129
  223.5 23.8 %project_qkv.5 = (bf16[3,16,3072,128]{3,2,1,0:T(8,128)(2,1)}, bf16[3,4,256,3072]{3,2,1,0:T(8,128)(2,1)}) custom-call(s32[1]{0:T(128)} %bitcast.me_ref, bf16[1,256,3072]{2,1,0:T(8,128)(2,1)} %collective-permute-done.4.x0, bf16[1,256,3072]{2,1,0:T(8,128)(2,1)} %collective-permute-done.5.x1, ...), custom_call_target="tpu_custom_call", output_to_operand_aliasing={{0}: (6, {}), {1}: (7, {})} | custom-call | flops 14495514624 | bytes 34603008 | tf_op jit(solution)/shard_map/project_qkv/pallas_call | solution.py:129
  247.3 24.0 %project_qkv.6 = (bf16[3,16,3072,128]{3,2,1,0:T(8,128)(2,1)}, bf16[3,4,256,3072]{3,2,1,0:T(8,128)(2,1)}) custom-call(s32[1]{0:T(128)} %bitcast.me_ref, bf16[1,256,3072]{2,1,0:T(8,128)(2,1)} %copy-done.1, bf16[1,256,3072]{2,1,0:T(8,128)(2,1)} %collective-permute-done.3.x1, bf16[3072,9216]{1,0:T(8,128)(2,1)} %w.7, ...), custom_call_target="tpu_custom_call", output_to_operand_aliasing={{0}: (6, {}), {1}: (7, {})} | custom-call | flops 14495514624 | bytes 34603008 | tf_op jit(solution)/shard_map/project_qkv/pallas_call | solution.py:129
  271.3 23.8 %project_qkv.7 = (bf16[3,16,3072,128]{3,2,1,0:T(8,128)(2,1)}, bf16[3,4,256,3072]{3,2,1,0:T(8,128)(2,1)}) custom-call(s32[1]{0:T(128)} %bitcast.me_ref, bf16[1,256,3072]{2,1,0:T(8,128)(2,1)} %copy-done, bf16[1,256,3072]{2,1,0:T(8,128)(2,1)} %collective-permute-done.1.x1, bf16[3072,9216]{1,0:T(8,128)(2,1)} %w.7, ...), custom_call_target="tpu_custom_call", output_to_operand_aliasing={{0}: (6, {}), {1}: (7, {})} | custom-call | flops 14495514624 | bytes 34603008 | tf_op jit(solution)/shard_map/project_qkv/pallas_call | solution.py:129
  295.1 11.0 %project_grad.5 = (bf16[16,3072,128]{2,1,0:T(8,128)(2,1)}, bf16[3,4,256,3072]{3,2,1,0:T(8,128)(2,1)}) custom-call(s32[1]{0:T(128)} %bitcast.me_ref, bf16[1,256,3072]{2,1,0:T(8,128)(2,1)} %collective-permute-done.11.x0, bf16[1,256,3072]{2,1,0:T(8,128)(2,1)} %collective-permute-done.12.x1, ...), custom_call_target="tpu_custom_call", output_to_operand_aliasing={{0}: (4, {}), {1}: (5, {})} | custom-call | flops 4831838208 | bytes 15728640 | tf_op jit(solution)/shard_map/project_grad/pallas_call | solution.py:129
  306.1 82.4 %attention.3 = (bf16[3,1024,1536]{2,1,0:T(8,128)(2,1)}, bf16[3,3,1024,1536]{3,2,1,0:T(8,128)(2,1)}) custom-call(bf16[3,16,3072,128]{3,2,1,0:T(8,128)(2,1)} %get-tuple-element.41.q.k.v, bf16[3,16,3072,128]{3,2,1,0:T(8,128)(2,1)} %get-tuple-element.41.q.k.v, bf16[3,16,3072,128]{3,2,1,0:T(8,128)(2,1)} %get-tuple-element.41.q.k.v, ...), custom_call_target="tpu_custom_call" | custom-call | flops 32212254720 | bytes 33554432 | tf_op jit(solution)/shard_map/attention/pallas_call | solution.py:224
  388.6 11.1 %project_grad.6 = (bf16[16,3072,128]{2,1,0:T(8,128)(2,1)}, bf16[3,4,256,3072]{3,2,1,0:T(8,128)(2,1)}) custom-call(s32[1]{0:T(128)} %bitcast.me_ref, bf16[1,256,3072]{2,1,0:T(8,128)(2,1)} %collective-permute-done.9.x0, bf16[1,256,3072]{2,1,0:T(8,128)(2,1)} %collective-permute-done.10.x1, ...), custom_call_target="tpu_custom_call", output_to_operand_aliasing={{0}: (4, {}), {1}: (5, {})} | custom-call | flops 4831838208 | bytes 15728640 | tf_op jit(solution)/shard_map/project_grad/pallas_call | solution.py:129
  399.6 82.1 %attention.4 = (bf16[3,1024,1536]{2,1,0:T(8,128)(2,1)}, bf16[3,3,1024,1536]{3,2,1,0:T(8,128)(2,1)}) custom-call(bf16[3,16,3072,128]{3,2,1,0:T(8,128)(2,1)} %get-tuple-element.41.q.k.v, bf16[3,16,3072,128]{3,2,1,0:T(8,128)(2,1)} %get-tuple-element.41.q.k.v, ...), custom_call_target="tpu_custom_call", output_to_operand_aliasing={{0}: (6, {}), {1}: (7, {})} | custom-call | flops 32212254720 | bytes 33554432 | tf_op jit(solution)/shard_map/attention/pallas_call | solution.py:224
  481.8 11.2 %project_grad.7 = (bf16[16,3072,128]{2,1,0:T(8,128)(2,1)}, bf16[3,4,256,3072]{3,2,1,0:T(8,128)(2,1)}) custom-call(s32[1]{0:T(128)} %bitcast.me_ref, bf16[1,256,3072]{2,1,0:T(8,128)(2,1)} %collective-permute-done.7.x0, bf16[1,256,3072]{2,1,0:T(8,128)(2,1)} %collective-permute-done.8.x1, ...), custom_call_target="tpu_custom_call", output_to_operand_aliasing={{0}: (4, {}), {1}: (5, {})} | custom-call | flops 4831838208 | bytes 15728640 | tf_op jit(solution)/shard_map/project_grad/pallas_call | solution.py:129
  493.0 82.0 %attention.5 = (bf16[3,1024,1536]{2,1,0:T(8,128)(2,1)}, bf16[3,3,1024,1536]{3,2,1,0:T(8,128)(2,1)}) custom-call(bf16[3,16,3072,128]{3,2,1,0:T(8,128)(2,1)} %get-tuple-element.41.q.k.v, bf16[3,16,3072,128]{3,2,1,0:T(8,128)(2,1)} %get-tuple-element.41.q.k.v, ...), custom_call_target="tpu_custom_call", output_to_operand_aliasing={{0}: (6, {}), {1}: (7, {})} | custom-call | flops 32212254720 | bytes 33554432 | tf_op jit(solution)/shard_map/attention/pallas_call | solution.py:224
  585.1 41.5 %weight_grad.4 = (f32[3072,9216]{1,0:T(8,128)}, f32[3072,1536]{1,0:T(8,128)}) custom-call(s32[1]{0:T(128)} %bitcast.me_ref, bf16[3072,3072]{1,0:T(8,128)(2,1)} %bitcast.31, bf16[3,3072,1536]{2,1,0:T(8,128)(2,1)} %bitcast.28), custom_call_target="tpu_custom_call" | custom-call | flops 28991029248 | bytes 84934656 | tf_op jit(solution)/shard_map/weight_grad/pallas_call | solution.py:253
  626.6 41.7 %weight_grad.5 = (f32[3072,9216]{1,0:T(8,128)}, f32[3072,1536]{1,0:T(8,128)}) custom-call(s32[1]{0:T(128)} %bitcast.me_ref, bf16[3072,3072]{1,0:T(8,128)(2,1)} %bitcast.32, bf16[3,3072,1536]{2,1,0:T(8,128)(2,1)} %bitcast.29, f32[3072,9216]{1,0:T(8,128)} %get-tuple-element.56.rest_0_), custom_call_target="tpu_custom_call", output_to_operand_aliasing={{0}: (3, {})} | custom-call | flops 28991029248 | bytes 84934656 | tf_op jit(solution)/shard_map/weight_grad/pallas_call | solution.py:253
  668.2 41.8 %weight_grad.6 = (f32[3072,9216]{1,0:T(8,128)}, f32[3072,1536]{1,0:T(8,128)}) custom-call(s32[1]{0:T(128)} %bitcast.me_ref, bf16[3072,3072]{1,0:T(8,128)(2,1)} %bitcast.33, bf16[3,3072,1536]{2,1,0:T(8,128)(2,1)} %bitcast.30, f32[3072,9216]{1,0:T(8,128)} %get-tuple-element.57.rest_0_), custom_call_target="tpu_custom_call", output_to_operand_aliasing={{0}: (3, {})} | custom-call | flops 28991029248 | bytes 84934656 | tf_op jit(solution)/shard_map/weight_grad/pallas_call | solution.py:253
  710.6 46.0 %weight_grad.7 = (f32[3072,3072]{1,0:T(8,128)}, f32[1536,3072]{1,0:T(8,128)}) custom-call(s32[1]{0:T(128)} %bitcast.me_ref, bf16[3072,1536]{1,0:T(8,128)(2,1)} %bitcast.40, bf16[3072,3072]{1,0:T(8,128)(2,1)} %bitcast.39), custom_call_target="tpu_custom_call" | custom-call | flops 28991029248 | bytes 94371840 | tf_op jit(solution)/shard_map/weight_grad/pallas_call | solution.py:253
  760.7 19.3 %fusion.14 = bf16[3,256,3072]{2,1,0:T(8,128)(2,1)} fusion(bf16[3,256,3072]{2,1,0:T(8,128)(2,1)S(1)} %bitcast.42, bf16[3072,3072,1]{1,0,2:T(8,128)(2,1)} %bitcast.38, bf16[3,256,1536]{2,1,0:T(8,128)(2,1)S(1)} %get-tuple-element.68, bf16[3,256,1536]{2,1,0:T(8,128)(2,1)S(1)} %get-tuple-element.67), kind=kOutput, calls=%fused_computation.17 | convolution fusion | flops 14512029696 | bytes 33030144 | tf_op jit(solution)/shard_map/btw,wd->btd/dot_general | solution.py:345
  806.8 55.4 %fusion.12 = (f32[3072]{0:T(1024)S(1)}, f32[3,256]{1,0:T(4,128)S(1)}, f32[3,256,3072]{2,1,0:T(8,128)}) fusion(bf16[3,256,3072]{2,1,0:T(8,128)(2,1)} %param.6, f32[3,256]{1,0:T(4,128)S(1)} %copy-done.5, f32[3072]{0:T(1024)S(1)} %copy-done.3, bf16[3,256,9216]{2,1,0:T(8,128)(2,1)} %bitcast_dynamic-update-slice_fusion, bf16[3072,9216]{1,0:T(8,128)(2,1)} %w.7), kind=kOutput, calls=%fused_computation.15 | convolution fusion | flops 43503054848 | bytes 84965376 | tf_op jit(solution)/shard_map/btw,dw->btd/dot_general | solution.py:359
  876.2 13.8 %place_part.4._ = f32[3072,9216]{1,0:T(8,128)} custom-call(s32[1]{0:T(128)} %bitcast.me_ref, f32[3072,1536]{1,0:T(8,128)} %collective-permute-done.18.part, f32[3072,9216]{1,0:T(8,128)} %get-tuple-element.61._), custom_call_target="tpu_custom_call", output_to_operand_aliasing={{}: (2, {})} | custom-call | flops 188743680 | bytes 37748736 | tf_op jit(solution)/shard_map/place_part/pallas_call | solution.py:274
  890.0 13.8 %place_part.5._ = f32[3072,9216]{1,0:T(8,128)} custom-call(s32[1]{0:T(128)} %bitcast.me_ref, f32[3072,1536]{1,0:T(8,128)} %collective-permute-done.17.part, f32[3072,9216]{1,0:T(8,128)} %place_part.4._), custom_call_target="tpu_custom_call", output_to_operand_aliasing={{}: (2, {})} | custom-call | flops 188743680 | bytes 37748736 | tf_op jit(solution)/shard_map/place_part/pallas_call | solution.py:274
  903.8 13.8 %place_part.6 = f32[3072,9216]{1,0:T(8,128)} custom-call(s32[1]{0:T(128)} %bitcast.me_ref, f32[3072,1536]{1,0:T(8,128)} %collective-permute-done.16.part, f32[3072,9216]{1,0:T(8,128)} %place_part.5._), custom_call_target="tpu_custom_call", output_to_operand_aliasing={{}: (2, {})} | custom-call | flops 188743680 | bytes 37748736 | tf_op jit(solution)/shard_map/place_part/pallas_call | solution.py:274
  917.7 13.9 %place_part.7 = f32[3072,3072]{1,0:T(8,128)} custom-call(s32[1]{0:T(128)} %bitcast.me_ref, f32[1536,3072]{1,0:T(8,128)} %collective-permute-done.19.part, f32[3072,3072]{1,0:T(8,128)} %get-tuple-element.64._), custom_call_target="tpu_custom_call", output_to_operand_aliasing={{}: (2, {})} | custom-call | flops 188743680 | bytes 37748736 | tf_op jit(solution)/shard_map/place_part/pallas_call | solution.py:274
  (85 shorter events, 102.4 us)
Async XLA Ops:
  11.1 112.9 %collective-permute-start.6 = (bf16[3,256,3072]{2,1,0:T(8,128)(2,1)}, bf16[3,256,3072]{2,1,0:T(8,128)(2,1)}, u32[]{:S(2)}, u32[]{:S(2)}) collective-permute-start(bf16[3,256,3072]{2,1,0:T(8,128)(2,1)} %fusion.6.x0), channel_id=1, source_target_pairs={{0,1},{1,0},{2,3},{3,2},{4,5},{5,4},{6,7},{7,6}} | collective-permute-start | bytes 14155784 | tf_op jit(solution)/shard_map/ppermute | solution.py:312
  16.6 37.9 %collective-permute-start = (bf16[1,256,3072]{2,1,0:T(8,128)(2,1)}, bf16[1,256,3072]{2,1,0:T(8,128)(2,1)S(1)}, u32[]{:S(2)}, u32[]{:S(2)}) collective-permute-start(bf16[1,256,3072]{2,1,0:T(8,128)(2,1)} %get-tuple-element.74), channel_id=1, source_target_pairs={{0,2},{1,3},{2,0},{3,1},{4,6},{5,7},{6,4},{7,5}} | collective-permute-start | bytes 4718600 | tf_op jit(solution)/shard_map/ppermute | solution.py:313
  19.1 69.2 %collective-permute-start.2 = (bf16[1,256,3072]{2,1,0:T(8,128)(2,1)}, bf16[1,256,3072]{2,1,0:T(8,128)(2,1)S(1)}, u32[]{:S(2)}, u32[]{:S(2)}) collective-permute-start(bf16[1,256,3072]{2,1,0:T(8,128)(2,1)} %get-tuple-element.73), channel_id=1, source_target_pairs={{0,2},{1,3},{2,0},{3,1},{4,6},{5,7},{6,4},{7,5}} | collective-permute-start | bytes 4718600 | tf_op jit(solution)/shard_map/ppermute | solution.py:313
  19.1 102.9 %collective-permute-start.4 = (bf16[1,256,3072]{2,1,0:T(8,128)(2,1)}, bf16[1,256,3072]{2,1,0:T(8,128)(2,1)}, u32[]{:S(2)}, u32[]{:S(2)}) collective-permute-start(bf16[1,256,3072]{2,1,0:T(8,128)(2,1)} %get-tuple-element.72), channel_id=1, source_target_pairs={{0,2},{1,3},{2,0},{3,1},{4,6},{5,7},{6,4},{7,5}} | collective-permute-start | bytes 4718600 | tf_op jit(solution)/shard_map/ppermute | solution.py:313
  21.1 166.2 %collective-permute-start.13 = (bf16[3,256,3072]{2,1,0:T(8,128)(2,1)}, bf16[3,256,3072]{2,1,0:T(8,128)(2,1)}, u32[]{:S(2)}, u32[]{:S(2)}) collective-permute-start(bf16[3,256,3072]{2,1,0:T(8,128)(2,1)} %x0.1), channel_id=1, source_target_pairs={{0,1},{1,0},{2,3},{3,2},{4,5},{5,4},{6,7},{7,6}} | collective-permute-start | bytes 14155784 | tf_op jit(solution)/shard_map/ppermute | solution.py:312
  54.6 157.9 %copy-start = (bf16[1,256,3072]{2,1,0:T(8,128)(2,1)}, bf16[1,256,3072]{2,1,0:T(8,128)(2,1)S(1)}, u32[]{:S(2)}) copy-start(bf16[1,256,3072]{2,1,0:T(8,128)(2,1)S(1)} %collective-permute-done.x0) | copy-start | bytes 4718596
  54.6 157.9 %collective-permute-start.11 = (bf16[1,256,3072]{2,1,0:T(8,128)(2,1)}, bf16[1,256,3072]{2,1,0:T(8,128)(2,1)}, u32[]{:S(2)}, u32[]{:S(2)}) collective-permute-start(bf16[1,256,3072]{2,1,0:T(8,128)(2,1)} %get-tuple-element.69), channel_id=1, source_target_pairs={{0,2},{1,3},{2,0},{3,1},{4,6},{5,7},{6,4},{7,5}} | collective-permute-start | bytes 4718600 | tf_op jit(solution)/shard_map/ppermute | solution.py:314
  88.3 99.1 %copy-start.1 = (bf16[1,256,3072]{2,1,0:T(8,128)(2,1)}, bf16[1,256,3072]{2,1,0:T(8,128)(2,1)S(1)}, u32[]{:S(2)}) copy-start(bf16[1,256,3072]{2,1,0:T(8,128)(2,1)S(1)} %collective-permute-done.2.x0) | copy-start | bytes 4718596
  88.3 124.3 %collective-permute-start.9 = (bf16[1,256,3072]{2,1,0:T(8,128)(2,1)}, bf16[1,256,3072]{2,1,0:T(8,128)(2,1)}, u32[]{:S(2)}, u32[]{:S(2)}) collective-permute-start(bf16[1,256,3072]{2,1,0:T(8,128)(2,1)} %get-tuple-element.70), channel_id=1, source_target_pairs={{0,2},{1,3},{2,0},{3,1},{4,6},{5,7},{6,4},{7,5}} | collective-permute-start | bytes 4718600 | tf_op jit(solution)/shard_map/ppermute | solution.py:314
  122.1 100.9 %collective-permute-start.7 = (bf16[1,256,3072]{2,1,0:T(8,128)(2,1)}, bf16[1,256,3072]{2,1,0:T(8,128)(2,1)}, u32[]{:S(2)}, u32[]{:S(2)}) collective-permute-start(bf16[1,256,3072]{2,1,0:T(8,128)(2,1)} %get-tuple-element.71), channel_id=1, source_target_pairs={{0,2},{1,3},{2,0},{3,1},{4,6},{5,7},{6,4},{7,5}} | collective-permute-start | bytes 4718600 | tf_op jit(solution)/shard_map/ppermute | solution.py:314
  124.1 98.9 %collective-permute-start.5 = (bf16[1,256,3072]{2,1,0:T(8,128)(2,1)}, bf16[1,256,3072]{2,1,0:T(8,128)(2,1)}, u32[]{:S(2)}, u32[]{:S(2)}) collective-permute-start(bf16[1,256,3072]{2,1,0:T(8,128)(2,1)} %collective-permute-done.4.x0), channel_id=1, source_target_pairs={{0,1},{1,0},{2,3},{3,2},{4,5},{5,4},{6,7},{7,6}} | collective-permute-start | bytes 4718600 | tf_op jit(solution)/shard_map/ppermute | solution.py:319
  187.3 60.0 %collective-permute-start.3 = (bf16[1,256,3072]{2,1,0:T(8,128)(2,1)S(1)}, bf16[1,256,3072]{2,1,0:T(8,128)(2,1)}, u32[]{:S(2)}, u32[]{:S(2)}) collective-permute-start(bf16[1,256,3072]{2,1,0:T(8,128)(2,1)S(1)} %collective-permute-done.2.x0), channel_id=1, source_target_pairs={{0,1},{1,0},{2,3},{3,2},{4,5},{5,4},{6,7},{7,6}} | collective-permute-start | bytes 4718600 | tf_op jit(solution)/shard_map/ppermute | solution.py:319
  212.4 58.8 %collective-permute-start.1 = (bf16[1,256,3072]{2,1,0:T(8,128)(2,1)S(1)}, bf16[1,256,3072]{2,1,0:T(8,128)(2,1)}, u32[]{:S(2)}, u32[]{:S(2)}) collective-permute-start(bf16[1,256,3072]{2,1,0:T(8,128)(2,1)S(1)} %collective-permute-done.x0), channel_id=1, source_target_pairs={{0,1},{1,0},{2,3},{3,2},{4,5},{5,4},{6,7},{7,6}} | collective-permute-start | bytes 4718600 | tf_op jit(solution)/shard_map/ppermute | solution.py:319
  212.5 82.6 %collective-permute-start.12 = (bf16[1,256,3072]{2,1,0:T(8,128)(2,1)}, bf16[1,256,3072]{2,1,0:T(8,128)(2,1)}, u32[]{:S(2)}, u32[]{:S(2)}) collective-permute-start(bf16[1,256,3072]{2,1,0:T(8,128)(2,1)} %collective-permute-done.11.x0), channel_id=1, source_target_pairs={{0,1},{1,0},{2,3},{3,2},{4,5},{5,4},{6,7},{7,6}} | collective-permute-start | bytes 4718600 | tf_op jit(solution)/shard_map/ppermute | solution.py:320
  223.0 165.5 %collective-permute-start.10 = (bf16[1,256,3072]{2,1,0:T(8,128)(2,1)}, bf16[1,256,3072]{2,1,0:T(8,128)(2,1)}, u32[]{:S(2)}, u32[]{:S(2)}) collective-permute-start(bf16[1,256,3072]{2,1,0:T(8,128)(2,1)} %collective-permute-done.9.x0), channel_id=1, source_target_pairs={{0,1},{1,0},{2,3},{3,2},{4,5},{5,4},{6,7},{7,6}} | collective-permute-start | bytes 4718600 | tf_op jit(solution)/shard_map/ppermute | solution.py:320
  223.0 258.7 %collective-permute-start.8 = (bf16[1,256,3072]{2,1,0:T(8,128)(2,1)}, bf16[1,256,3072]{2,1,0:T(8,128)(2,1)}, u32[]{:S(2)}, u32[]{:S(2)}) collective-permute-start(bf16[1,256,3072]{2,1,0:T(8,128)(2,1)} %collective-permute-done.7.x0), channel_id=1, source_target_pairs={{0,1},{1,0},{2,3},{3,2},{4,5},{5,4},{6,7},{7,6}} | collective-permute-start | bytes 4718600 | tf_op jit(solution)/shard_map/ppermute | solution.py:320
  578.2 178.4 %collective-permute-start.14 = (bf16[3,256,1536]{2,1,0:T(8,128)(2,1)}, bf16[3,256,1536]{2,1,0:T(8,128)(2,1)}, u32[]{:S(2)}, u32[]{:S(2)}) collective-permute-start(bf16[3,256,1536]{2,1,0:T(8,128)(2,1)} %constant_dynamic-slice_fusion.1), channel_id=1, source_target_pairs={{0,1},{1,0},{2,3},{3,2},{4,5},{5,4},{6,7},{7,6}} | collective-permute-start | bytes 7077896 | tf_op jit(solution)/shard_map/ppermute | solution.py:334
  584.6 195.4 %collective-permute-start.15 = (bf16[3,3,256,1536]{3,2,1,0:T(8,128)(2,1)}, bf16[3,3,256,1536]{3,2,1,0:T(8,128)(2,1)}, u32[]{:S(2)}, u32[]{:S(2)}) collective-permute-start(bf16[3,3,256,1536]{3,2,1,0:T(8,128)(2,1)} %constant_dynamic-slice_fusion), channel_id=1, source_target_pairs={{0,1},{1,0},{2,3},{3,2},{4,5},{5,4},{6,7},{7,6}} | collective-permute-start | bytes 21233672 | tf_op jit(solution)/shard_map/ppermute | solution.py:334
  710.0 193.8 %collective-permute-start.16 = (f32[3072,1536]{1,0:T(8,128)}, f32[3072,1536]{1,0:T(8,128)}, u32[]{:S(2)}, u32[]{:S(2)}) collective-permute-start(f32[3072,1536]{1,0:T(8,128)} %get-tuple-element.58), channel_id=1, source_target_pairs={{0,1},{1,0},{2,3},{3,2},{4,5},{5,4},{6,7},{7,6}} | collective-permute-start | bytes 56623112 | tf_op jit(solution)/shard_map/ppermute | solution.py:353
  710.1 180.0 %collective-permute-start.17 = (f32[3072,1536]{1,0:T(8,128)}, f32[3072,1536]{1,0:T(8,128)}, u32[]{:S(2)}, u32[]{:S(2)}) collective-permute-start(f32[3072,1536]{1,0:T(8,128)} %get-tuple-element.59), channel_id=1, source_target_pairs={{0,1},{1,0},{2,3},{3,2},{4,5},{5,4},{6,7},{7,6}} | collective-permute-start | bytes 56623112 | tf_op jit(solution)/shard_map/ppermute | solution.py:353
  710.5 165.7 %collective-permute-start.18 = (f32[3072,1536]{1,0:T(8,128)}, f32[3072,1536]{1,0:T(8,128)}, u32[]{:S(2)}, u32[]{:S(2)}) collective-permute-start(f32[3072,1536]{1,0:T(8,128)} %get-tuple-element.60), channel_id=1, source_target_pairs={{0,1},{1,0},{2,3},{3,2},{4,5},{5,4},{6,7},{7,6}} | collective-permute-start | bytes 56623112 | tf_op jit(solution)/shard_map/ppermute | solution.py:353
  756.6 161.1 %collective-permute-start.19 = (f32[1536,3072]{1,0:T(8,128)}, f32[1536,3072]{1,0:T(8,128)}, u32[]{:S(2)}, u32[]{:S(2)}) collective-permute-start(f32[1536,3072]{1,0:T(8,128)} %get-tuple-element.63), channel_id=1, source_target_pairs={{0,1},{1,0},{2,3},{3,2},{4,5},{5,4},{6,7},{7,6}} | collective-permute-start | bytes 56623112 | tf_op jit(solution)/shard_map/ppermute | solution.py:341
  862.2 1.2 collective-permute-start.20
  863.4 12.2 %collective-permute-start.21 = (f32[3072]{0:T(1024)S(1)}, f32[3072]{0:T(1024)S(1)}, u32[]{:S(2)}, u32[]{:S(2)}) collective-permute-start(f32[3072]{0:T(1024)S(1)} %add.41), channel_id=1, source_target_pairs={{0,2},{1,3},{2,0},{3,1},{4,6},{5,7},{6,4},{7,5}} | collective-permute-start | bytes 36872 | tf_op jit(solution)/shard_map/ppermute | solution.py:366
  (7 other events, 78.1 us)

commit v2 on v1

--- a/solution.py
+++ b/solution.py
@@ -244,7 +244,7 @@
     mine[...] = vals
 
 
-def weight_grad(me, lhs, rhs, full_shape, place, buf, part=None, blk_r=512, blk_c=768):
+def weight_grad(me, lhs, rhs, full_shape, place, buf, part=None, blk_r=256, blk_c=1536):
     tok, n_r = lhs.shape
     n_c = rhs.shape[-1]
     rhs_spec = pl.BlockSpec((tok, blk_c), lambda j, i, m: (0, j)) if part is None else pl.BlockSpec((None, tok, blk_c), lambda j, i, m: (part, 0, j))
@@ -265,24 +265,54 @@
     )(me, lhs, rhs, *bufs)
 
 
-def place_kernel(me_ref, part, _, full):
-    full[...] = part[...]
-
-
-def place_part(me, part, full, place, blk_r=512, blk_c=1536):
-    n_r, n_c = part.shape
+def dnormed_kernel(me_ref, mine, theirs, w, *rest):
+    r_qkv, r_o, (out, g_qkv, g_o, sems) = rest[:3], rest[3], rest[-4:]
+    step = pl.program_id(0)
+    core = lax.rem(me_ref[0], 2)
+    n_batch, tok, wid = mine.shape[1:]
+    rows = w.shape[0]
+    copies = []
+    for part, ref in enumerate(r_qkv):
+        at = g_qkv.at[pl.ds(step * rows, rows), pl.ds(pl.multiple_of((2 * part + 1 - core) * wid, LANES), wid)]
+        copies.append(pltpu.make_async_copy(ref, at, sems.at[part]))
+    rows_o = r_o.shape[0]
+    copies.append(pltpu.make_async_copy(r_o, g_o.at[pl.ds((1 - core) * wid + step * rows_o, rows_o), :], sems.at[3]))
+    for copy in copies:
+        copy.start()
+    acc = None
+    for part in range(3):
+        for ref, side in ((mine, core), (theirs, 1 - core)):
+            cols = pl.ds(pl.multiple_of((2 * part + side) * wid, LANES), wid)
+            term = lax.dot_general(ref[part].reshape(n_batch * tok, wid), w[:, cols], (((1,), (1,)), ((), ())), preferred_element_type=jnp.float32)
+            acc = term if acc is None else acc + term
+    out[...] = acc.reshape(out.shape)
+    for copy in copies:
+        copy.wait()
+
+
+def grad_normed_and_place(me, fused, recv_f, w_qkv, recv, recv_o, g_qkv, g_o):
+    _, n_batch, tok, wid = recv_f.shape
+    d = w_qkv.shape[0]
+    steps = 12
+    rows, rows_o = d // steps, wid // steps
+    once = pl.Buffered(buffer_count=1)
+    f_spec = lambda at: pl.BlockSpec((3, n_batch, tok, wid), lambda i, m: (0, 0, at(m), 0), pipeline_mode=once)
+    r_spec = pl.BlockSpec((rows, wid), lambda i, m: (i, 0))
     return pl.pallas_call(
-        place_kernel,
+        dnormed_kernel,
         grid_spec=pltpu.PrefetchScalarGridSpec(
-            num_scalar_prefetch=1, grid=(n_c // blk_c, n_r // blk_r),
-            in_specs=[pl.BlockSpec((blk_r, blk_c), lambda j, i, m: (i, j)), ANY],
-            out_specs=pl.BlockSpec((blk_r, blk_c), lambda j, i, m: place(i, j, 1 - lax.rem(m[0], 2)))),
-        out_shape=jax.ShapeDtypeStruct(full.shape, jnp.float32),
-        input_output_aliases={2: 0},
-        compiler_params=params(("arbitrary", "arbitrary")),
-        cost_estimate=cost(n_r * n_c * 40, 8 * n_r * n_c),
-        name="place_part",
-    )(me, part, full)
+            num_scalar_prefetch=1, grid=(steps,),
+            in_specs=[f_spec(lambda m: m[0]), f_spec(lambda m: 0), pl.BlockSpec((rows, 6 * wid), lambda i, m: (i, 0)),
+                      r_spec, r_spec, r_spec, pl.BlockSpec((rows_o, d), lambda i, m: (i, 0)), ANY, ANY],
+            out_specs=[pl.BlockSpec((n_batch, tok, rows), lambda i, m: (0, 0, i)), ANY, ANY],
+            scratch_shapes=[pltpu.SemaphoreType.DMA((4,))]),
+        out_shape=[jax.ShapeDtypeStruct((n_batch, tok, d), jnp.float32),
+                   jax.ShapeDtypeStruct(g_qkv.shape, jnp.float32), jax.ShapeDtypeStruct(g_o.shape, jnp.float32)],
+        input_output_aliases={8: 1, 9: 2},
+        compiler_params=params(("arbitrary",)),
+        cost_estimate=cost(2 * n_batch * tok * d * 6 * wid, 12 * wid * d + 8 * d * wid * 4),
+        name="grad_normed",
+    )(me, fused, recv_f, w_qkv, *recv, recv_o, g_qkv, g_o)
 
 
 def solution(mesh):
@@ -329,14 +359,14 @@
         grad_out_all = grd[1].reshape(n_batch * seq, d)
 
         def own_tokens(vals, axis):
-            mine = lax.dynamic_slice_in_dim(vals, index * tok, tok, axis)
             theirs = lax.dynamic_slice_in_dim(vals, partner * tok, tok, axis)
-            return mine, to_core(theirs)
-
-        a_mine, a_recv = own_tokens(attn, 1)
-        f_mine, f_recv = own_tokens(grad_fused, 2)
-
-        place_o = lambda i, j, c: (c * (wid // 512) + i, j)
+            return to_core(theirs)
+
+        a_mine = lax.dynamic_slice_in_dim(attn, index * tok, tok, 1)
+        a_recv = own_tokens(attn, 1)
+        f_recv = own_tokens(grad_fused, 2)
+
+        place_o = lambda i, j, c: (c * (wid // 256) + i, j)
         g_wo, mine_wo = weight_grad(me, attn.reshape(n_batch * seq, wid), grad_out_all, (2 * wid, d), place_o, None)
         recv_wo = to_core(mine_wo)
 
@@ -348,15 +378,11 @@
         g_wqkv, recv = None, []
         fused_tok = grad_fused.reshape(3, n_batch * seq, wid)
         for part in range(3):
-            place_p = lambda i, j, c, part=part: (i, part * 4 + c * 2 + j)
+            place_p = lambda i, j, c, part=part: (i, part * 2 + c)
             g_wqkv, mine = weight_grad(me, normed_all, fused_tok, (d, 6 * wid), place_p, g_wqkv, part)
             recv.append(to_core(mine))
 
-        pieces = []
-        for part in range(3):
-            pieces += [jnp.where(even, f_mine[part], f_recv[part]), jnp.where(even, f_recv[part], f_mine[part])]
-        fused_local = jnp.concatenate(pieces, axis=-1)
-        grad_normed = jnp.einsum('btw,dw->btd', fused_local, w_qkv, preferred_element_type=jnp.float32)
+        grad_normed, g_wqkv, g_wo = grad_normed_and_place(me, grad_fused, f_recv, w_qkv, recv, recv_wo, g_wqkv, g_wo)
         unit_rows = hidden_f * inv_rms
         grad_unit = grad_normed * gain
         mean_dot = jnp.mean(grad_unit * unit_rows, axis=-1, keepdims=True)
@@ -364,10 +390,6 @@
         g_norm = jnp.sum(grad_normed * unit_rows, axis=(0, 1))
         g_norm = g_norm + to_core(g_norm)
         g_norm = g_norm + to_chip(g_norm)
-
-        g_wo = place_part(me, recv_wo, g_wo, lambda i, j, c: (c * (wid // 512) + i, j))
-        for part in range(3):
-            g_wqkv = place_part(me, recv[part], g_wqkv, lambda i, j, c, part=part: (i, part * 2 + c))
         return (block_out, grad_hidden, g_wqkv, g_wo.reshape(n_heads, head_dim, d), g_norm)
 
     tok_spec = P('dp', 'sp', None)

time: 939 us -> 891 us (0.949)
  matrix products: 74.6 us -> 19 us
  other arithmetic: 55.1 us -> 30.7 us
  waiting for transfers between devices: 99.9 us -> 123 us
  Pallas kernels: 665 us -> 677 us
    dot_general x1 -> x0, matrix products: 55.4 us -> none  [device_step(): jnp.einsum('btw,dw->btd', fused_local, w_qkv, preferred_element_type=jnp....]
    ppermute x3, waiting for transfers between devices: 10 us -> 41.9 us  [device_step(): far_g = [to_chip(grad_out[b:b + 1]) for b in range(n_batch)]]
    ppermute x3, waiting for transfers between devices: 88.8 us -> 57.1 us  [device_step(): far_n = [to_chip(normed[b:b + 1]) for b in range(n_batch)]]
    pallas_call x4 -> x1, Pallas kernels: 55.3 us -> 82.7 us  [grad_normed_and_place(): pl.pallas_call(dnormed_kernel, grid_spec=pltpu.PrefetchScalarGridSpec(num...]
    ppermute x2, waiting for transfers between devices: 0.01 us -> 23.2 us  [own_tokens(): return to_core(theirs)]
    unnamed x6 -> x2, other arithmetic: 22.4 us -> 0.01 us
    pallas_call x4, Pallas kernels: 171 us -> 155 us  [weight_grad(): pl.pallas_call(wgrad_kernel, grid_spec=pltpu.PrefetchScalarGridSpec(num_s...]
  transfers between devices with their start and end apart: 22 -> 22, of which waited for: 5 -> 6; matrix products, arithmetic and copies ran while one was open for 15% -> 6% of each run, Pallas kernels for 60% -> 52%
where the time goes in v2:
time: 891 us; the launch traced here: 885 us
  Pallas kernels  677 us (76%)
  waiting for transfers between devices  123 us (14%)
  other arithmetic  30.7 us (3%)
  matrix products  19 us (2%)
  local copies, waits for them, and re-layouts  18.3 us (2%)
  starting transfers between devices  16.2 us (2%)
    pallas_call x3, Pallas kernels, attention(): pl.pallas_call(functools.partial(attn_kernel, head_dim), grid=(heads_mine...  246 us
    pallas_call x8, Pallas kernels, project(): pl.pallas_call(functools.partial(proj_kernel, rope, heads_blk, head_dim),...  192 us
    pallas_call x4, Pallas kernels, weight_grad(): pl.pallas_call(wgrad_kernel, grid_spec=pltpu.PrefetchScalarGridSpec(num_s...  155 us
    pallas_call x1, Pallas kernels, grad_normed_and_place(): pl.pallas_call(dnormed_kernel, grid_spec=pltpu.PrefetchScalarGridSpec(num...  82.7 us
    ppermute x3, waiting for transfers between devices, device_step(): far_n = [to_chip(normed[b:b + 1]) for b in range(n_batch)]  57.1 us
    ppermute x3, waiting for transfers between devices, device_step(): far_g = [to_chip(grad_out[b:b + 1]) for b in range(n_batch)]  41.9 us
    ppermute x2, waiting for transfers between devices, own_tokens(): return to_core(theirs)  23.2 us
    dot_general x1, matrix products, device_step(): jnp.einsum('btw,wd->btd', attn_local, w_out2, preferred_element_type=jnp....  19 us
  transfers between devices with their start and end apart: 22, of which 6 were waited for; matrix products, arithmetic and copies ran while one was open for 6% of the time, Pallas kernels for 52%

profile of v2, /device:TPU:0, one launch (start us, length us, event | category | flops | bytes accessed | tf_op | source)
XLA Modules:
  0.0 885.2 jit_solution(18446187739675767680)
XLA Ops:
  29.2 25.4 %collective-permute-done.4.x0 = bf16[1,256,3072]{2,1,0:T(8,128)(2,1)S(1)} collective-permute-done((bf16[1,256,3072]{2,1,0:T(8,128)(2,1)}, bf16[1,256,3072]{2,1,0:T(8,128)(2,1)S(1)}, u32[]{:S(2)}, u32[]{:S(2)}) %collective-permute-start.4) | collective-permute-done | bytes 1572896 | tf_op jit(solution)/shard_map/ppermute | solution.py:343
  56.6 31.7 %collective-permute-done.2.x0 = bf16[1,256,3072]{2,1,0:T(8,128)(2,1)S(1)} collective-permute-done((bf16[1,256,3072]{2,1,0:T(8,128)(2,1)}, bf16[1,256,3072]{2,1,0:T(8,128)(2,1)S(1)}, u32[]{:S(2)}, u32[]{:S(2)}) %collective-permute-start.2) | collective-permute-done | bytes 1572896 | tf_op jit(solution)/shard_map/ppermute | solution.py:343
  90.3 31.8 %collective-permute-done.11.x0 = bf16[1,256,3072]{2,1,0:T(8,128)(2,1)} collective-permute-done((bf16[1,256,3072]{2,1,0:T(8,128)(2,1)}, bf16[1,256,3072]{2,1,0:T(8,128)(2,1)}, u32[]{:S(2)}, u32[]{:S(2)}) %collective-permute-start.11) | collective-permute-done | bytes 1572896 | tf_op jit(solution)/shard_map/ppermute | solution.py:344
  124.7 62.5 %project_qkv.4 = (bf16[3,16,3072,128]{3,2,1,0:T(8,128)(2,1)}, bf16[3,4,256,3072]{3,2,1,0:T(8,128)(2,1)}) custom-call(s32[1]{0:T(128)} %bitcast.me_ref, bf16[3,256,3072]{2,1,0:T(8,128)(2,1)} %fusion.4.x0, bf16[3,256,3072]{2,1,0:T(8,128)(2,1)} %collective-permute-done.6.x1, bf16[3072,9216]{1,0:T(8,128)(2,1)} %w.9, ...), custom_call_target="tpu_custom_call" | custom-call | flops 43486543872 | bytes 103809024 | tf_op jit(solution)/shard_map/project_qkv/pallas_call | solution.py:129
  187.8 24.6 %project_grad.4 = (bf16[16,3072,128]{2,1,0:T(8,128)(2,1)}, bf16[3,4,256,3072]{3,2,1,0:T(8,128)(2,1)}) custom-call(s32[1]{0:T(128)} %bitcast.me_ref, bf16[3,256,3072]{2,1,0:T(8,128)(2,1)} %x0.1, bf16[3,256,3072]{2,1,0:T(8,128)(2,1)} %collective-permute-done.13.x1, bf16[3072,3072]{1,0:T(8,128)(2,1)} %bitcast.16, ...), custom_call_target="tpu_custom_call" | custom-call | flops 14495514624 | bytes 47185920 | tf_op jit(solution)/shard_map/project_grad/pallas_call | solution.py:129
  212.9 10.1 %collective-permute-done.7.x0 = bf16[1,256,3072]{2,1,0:T(8,128)(2,1)} collective-permute-done((bf16[1,256,3072]{2,1,0:T(8,128)(2,1)}, bf16[1,256,3072]{2,1,0:T(8,128)(2,1)}, u32[]{:S(2)}, u32[]{:S(2)}) %collective-permute-start.7) | collective-permute-done | bytes 1572896 | tf_op jit(solution)/shard_map/ppermute | solution.py:344
  223.5 23.7 %project_qkv.5 = (bf16[3,16,3072,128]{3,2,1,0:T(8,128)(2,1)}, bf16[3,4,256,3072]{3,2,1,0:T(8,128)(2,1)}) custom-call(s32[1]{0:T(128)} %bitcast.me_ref, bf16[1,256,3072]{2,1,0:T(8,128)(2,1)} %copy-done.2, bf16[1,256,3072]{2,1,0:T(8,128)(2,1)} %collective-permute-done.5.x1, bf16[3072,9216]{1,0:T(8,128)(2,1)} %w.9, ...), custom_call_target="tpu_custom_call", output_to_operand_aliasing={{0}: (6, {}), {1}: (7, {})} | custom-call | flops 14495514624 | bytes 34603008 | tf_op jit(solution)/shard_map/project_qkv/pallas_call | solution.py:129
  247.2 11.1 %project_grad.5 = (bf16[16,3072,128]{2,1,0:T(8,128)(2,1)}, bf16[3,4,256,3072]{3,2,1,0:T(8,128)(2,1)}) custom-call(s32[1]{0:T(128)} %bitcast.me_ref, bf16[1,256,3072]{2,1,0:T(8,128)(2,1)} %collective-permute-done.11.x0, bf16[1,256,3072]{2,1,0:T(8,128)(2,1)} %collective-permute-done.12.x1, ...), custom_call_target="tpu_custom_call", output_to_operand_aliasing={{0}: (4, {}), {1}: (5, {})} | custom-call | flops 4831838208 | bytes 15728640 | tf_op jit(solution)/shard_map/project_grad/pallas_call | solution.py:129
  258.3 24.3 %project_qkv.6 = (bf16[3,16,3072,128]{3,2,1,0:T(8,128)(2,1)}, bf16[3,4,256,3072]{3,2,1,0:T(8,128)(2,1)}) custom-call(s32[1]{0:T(128)} %bitcast.me_ref, bf16[1,256,3072]{2,1,0:T(8,128)(2,1)} %copy-done.1, bf16[1,256,3072]{2,1,0:T(8,128)(2,1)} %collective-permute-done.3.x1, bf16[3072,9216]{1,0:T(8,128)(2,1)} %w.9, ...), custom_call_target="tpu_custom_call", output_to_operand_aliasing={{0}: (6, {}), {1}: (7, {})} | custom-call | flops 14495514624 | bytes 34603008 | tf_op jit(solution)/shard_map/project_qkv/pallas_call | solution.py:129
  282.7 23.7 %project_qkv.7 = (bf16[3,16,3072,128]{3,2,1,0:T(8,128)(2,1)}, bf16[3,4,256,3072]{3,2,1,0:T(8,128)(2,1)}) custom-call(s32[1]{0:T(128)} %bitcast.me_ref, bf16[1,256,3072]{2,1,0:T(8,128)(2,1)} %collective-permute-done.x0, bf16[1,256,3072]{2,1,0:T(8,128)(2,1)} %collective-permute-done.1.x1, ...), custom_call_target="tpu_custom_call", output_to_operand_aliasing={{0}: (6, {}), {1}: (7, {})} | custom-call | flops 14495514624 | bytes 34603008 | tf_op jit(solution)/shard_map/project_qkv/pallas_call | solution.py:129
  306.4 82.0 %attention.3 = (bf16[3,1024,1536]{2,1,0:T(8,128)(2,1)}, bf16[3,3,1024,1536]{3,2,1,0:T(8,128)(2,1)}) custom-call(bf16[3,16,3072,128]{3,2,1,0:T(8,128)(2,1)} %get-tuple-element.44.q.k.v, bf16[3,16,3072,128]{3,2,1,0:T(8,128)(2,1)} %get-tuple-element.44.q.k.v, bf16[3,16,3072,128]{3,2,1,0:T(8,128)(2,1)} %get-tuple-element.44.q.k.v, ...), custom_call_target="tpu_custom_call" | custom-call | flops 32212254720 | bytes 33554432 | tf_op jit(solution)/shard_map/attention/pallas_call | solution.py:224
  388.4 11.3 %project_grad.6 = (bf16[16,3072,128]{2,1,0:T(8,128)(2,1)}, bf16[3,4,256,3072]{3,2,1,0:T(8,128)(2,1)}) custom-call(s32[1]{0:T(128)} %bitcast.me_ref, bf16[1,256,3072]{2,1,0:T(8,128)(2,1)} %collective-permute-done.9.x0, bf16[1,256,3072]{2,1,0:T(8,128)(2,1)} %collective-permute-done.10.x1, ...), custom_call_target="tpu_custom_call", output_to_operand_aliasing={{0}: (4, {}), {1}: (5, {})} | custom-call | flops 4831838208 | bytes 15728640 | tf_op jit(solution)/shard_map/project_grad/pallas_call | solution.py:129
  399.6 82.1 %attention.4 = (bf16[3,1024,1536]{2,1,0:T(8,128)(2,1)}, bf16[3,3,1024,1536]{3,2,1,0:T(8,128)(2,1)}) custom-call(bf16[3,16,3072,128]{3,2,1,0:T(8,128)(2,1)} %get-tuple-element.44.q.k.v, bf16[3,16,3072,128]{3,2,1,0:T(8,128)(2,1)} %get-tuple-element.44.q.k.v, ...), custom_call_target="tpu_custom_call", output_to_operand_aliasing={{0}: (6, {}), {1}: (7, {})} | custom-call | flops 32212254720 | bytes 33554432 | tf_op jit(solution)/shard_map/attention/pallas_call | solution.py:224
  481.7 11.1 %project_grad.7 = (bf16[16,3072,128]{2,1,0:T(8,128)(2,1)}, bf16[3,4,256,3072]{3,2,1,0:T(8,128)(2,1)}) custom-call(s32[1]{0:T(128)} %bitcast.me_ref, bf16[1,256,3072]{2,1,0:T(8,128)(2,1)} %collective-permute-done.7.x0, bf16[1,256,3072]{2,1,0:T(8,128)(2,1)} %collective-permute-done.8.x1, ...), custom_call_target="tpu_custom_call", output_to_operand_aliasing={{0}: (4, {}), {1}: (5, {})} | custom-call | flops 4831838208 | bytes 15728640 | tf_op jit(solution)/shard_map/project_grad/pallas_call | solution.py:129
  492.8 82.2 %attention.5 = (bf16[3,1024,1536]{2,1,0:T(8,128)(2,1)}, bf16[3,3,1024,1536]{3,2,1,0:T(8,128)(2,1)}) custom-call(bf16[3,16,3072,128]{3,2,1,0:T(8,128)(2,1)} %get-tuple-element.44.q.k.v, bf16[3,16,3072,128]{3,2,1,0:T(8,128)(2,1)} %get-tuple-element.44.q.k.v, ...), custom_call_target="tpu_custom_call", output_to_operand_aliasing={{0}: (6, {}), {1}: (7, {})} | custom-call | flops 32212254720 | bytes 33554432 | tf_op jit(solution)/shard_map/attention/pallas_call | solution.py:224
  575.0 41.7 %weight_grad.7 = (f32[3072,3072]{1,0:T(8,128)}, f32[1536,3072]{1,0:T(8,128)}) custom-call(s32[1]{0:T(128)} %bitcast.me_ref, bf16[3072,1536]{1,0:T(8,128)(2,1)} %bitcast.26, bf16[3072,3072]{1,0:T(8,128)(2,1)} %bitcast.21), custom_call_target="tpu_custom_call" | custom-call | flops 28991029248 | bytes 75497472 | tf_op jit(solution)/shard_map/weight_grad/pallas_call | solution.py:253
  616.7 37.8 %weight_grad.4 = (f32[3072,9216]{1,0:T(8,128)}, f32[3072,1536]{1,0:T(8,128)}) custom-call(s32[1]{0:T(128)} %bitcast.me_ref, bf16[3072,3072]{1,0:T(8,128)(2,1)} %bitcast.13, bf16[3,3072,1536]{2,1,0:T(8,128)(2,1)} %bitcast.10), custom_call_target="tpu_custom_call" | custom-call | flops 28991029248 | bytes 66060288 | tf_op jit(solution)/shard_map/weight_grad/pallas_call | solution.py:253
  654.9 37.8 %weight_grad.5 = (f32[3072,9216]{1,0:T(8,128)}, f32[3072,1536]{1,0:T(8,128)}) custom-call(s32[1]{0:T(128)} %bitcast.me_ref, bf16[3072,3072]{1,0:T(8,128)(2,1)} %bitcast.14, bf16[3,3072,1536]{2,1,0:T(8,128)(2,1)} %bitcast.11, f32[3072,9216]{1,0:T(8,128)} %get-tuple-element.60.rest_0_), custom_call_target="tpu_custom_call", output_to_operand_aliasing={{0}: (3, {})} | custom-call | flops 28991029248 | bytes 66060288 | tf_op jit(solution)/shard_map/weight_grad/pallas_call | solution.py:253
  692.8 37.9 %weight_grad.6 = (f32[3072,9216]{1,0:T(8,128)}, f32[3072,1536]{1,0:T(8,128)}) custom-call(s32[1]{0:T(128)} %bitcast.me_ref, bf16[3072,3072]{1,0:T(8,128)(2,1)} %bitcast.15, bf16[3,3072,1536]{2,1,0:T(8,128)(2,1)} %bitcast.12, f32[3072,9216]{1,0:T(8,128)} %get-tuple-element.62.rest_0_), custom_call_target="tpu_custom_call", output_to_operand_aliasing={{0}: (3, {})} | custom-call | flops 28991029248 | bytes 66060288 | tf_op jit(solution)/shard_map/weight_grad/pallas_call | solution.py:253
  739.4 23.2 %collective-permute-done.14 = bf16[3,256,1536]{2,1,0:T(8,128)(2,1)S(1)} collective-permute-done((bf16[3,256,1536]{2,1,0:T(8,128)(2,1)S(1)}, bf16[3,256,1536]{2,1,0:T(8,128)(2,1)S(1)}, u32[]{:S(2)}, u32[]{:S(2)}) %collective-permute-start.14) | collective-permute-done | bytes 2359328 | tf_op jit(solution)/shard_map/ppermute | solution.py:363
  765.9 19.0 %fusion.12 = bf16[3,256,3072]{2,1,0:T(8,128)(2,1)} fusion(bf16[3,256,3072]{2,1,0:T(8,128)(2,1)S(1)} %bitcast.23, bf16[3072,3072,1]{1,0,2:T(8,128)(2,1)} %bitcast.20, bf16[3,256,1536]{2,1,0:T(8,128)(2,1)S(1)} %get-tuple-element.74, bf16[3,256,1536]{2,1,0:T(8,128)(2,1)S(1)} %get-tuple-element.73), kind=kOutput, calls=%fused_computation.15 | convolution fusion | flops 14512029696 | bytes 33030144 | tf_op jit(solution)/shard_map/btw,wd->btd/dot_general | solution.py:375
  785.0 82.7 %grad_normed.1 = (f32[3,256,3072]{2,1,0:T(8,128)}, f32[3072,9216]{1,0:T(8,128)}, f32[3072,3072]{1,0:T(8,128)}) custom-call(s32[1]{0:T(128)} %bitcast.me_ref, bf16[3,3,1024,1536]{3,2,1,0:T(8,128)(2,1)} %get-tuple-element.57.mine, bf16[3,3,256,1536]{3,2,1,0:T(8,128)(2,1)} %collective-permute-done.15.theirs, ...), custom_call_target="tpu_custom_call", output_to_operand_aliasing={{1}: (8, {}), {2}: (9, {})} | custom-call | flops 43486543872 | bytes 207618048 | tf_op jit(solution)/shard_map/grad_normed/pallas_call | solution.py:301
  867.7 6.6 fusion.10
  877.2 7.0 fusion.9
  (83 shorter events, 52.7 us)
Async XLA Ops:
  11.1 113.0 %collective-permute-start.6 = (bf16[3,256,3072]{2,1,0:T(8,128)(2,1)}, bf16[3,256,3072]{2,1,0:T(8,128)(2,1)}, u32[]{:S(2)}, u32[]{:S(2)}) collective-permute-start(bf16[3,256,3072]{2,1,0:T(8,128)(2,1)} %fusion.4.x0), channel_id=1, source_target_pairs={{0,1},{1,0},{2,3},{3,2},{4,5},{5,4},{6,7},{7,6}} | collective-permute-start | bytes 14155784 | tf_op jit(solution)/shard_map/ppermute | solution.py:342
  16.6 37.9 %collective-permute-start.4 = (bf16[1,256,3072]{2,1,0:T(8,128)(2,1)}, bf16[1,256,3072]{2,1,0:T(8,128)(2,1)S(1)}, u32[]{:S(2)}, u32[]{:S(2)}) collective-permute-start(bf16[1,256,3072]{2,1,0:T(8,128)(2,1)} %get-tuple-element.78), channel_id=1, source_target_pairs={{0,2},{1,3},{2,0},{3,1},{4,6},{5,7},{6,4},{7,5}} | collective-permute-start | bytes 4718600 | tf_op jit(solution)/shard_map/ppermute | solution.py:343
  19.1 69.2 %collective-permute-start.2 = (bf16[1,256,3072]{2,1,0:T(8,128)(2,1)}, bf16[1,256,3072]{2,1,0:T(8,128)(2,1)S(1)}, u32[]{:S(2)}, u32[]{:S(2)}) collective-permute-start(bf16[1,256,3072]{2,1,0:T(8,128)(2,1)} %get-tuple-element.79), channel_id=1, source_target_pairs={{0,2},{1,3},{2,0},{3,1},{4,6},{5,7},{6,4},{7,5}} | collective-permute-start | bytes 4718600 | tf_op jit(solution)/shard_map/ppermute | solution.py:343
  23.7 98.3 %collective-permute-start.11 = (bf16[1,256,3072]{2,1,0:T(8,128)(2,1)}, bf16[1,256,3072]{2,1,0:T(8,128)(2,1)}, u32[]{:S(2)}, u32[]{:S(2)}) collective-permute-start(bf16[1,256,3072]{2,1,0:T(8,128)(2,1)} %get-tuple-element.75), channel_id=1, source_target_pairs={{0,2},{1,3},{2,0},{3,1},{4,6},{5,7},{6,4},{7,5}} | collective-permute-start | bytes 4718600 | tf_op jit(solution)/shard_map/ppermute | solution.py:344
  25.7 161.5 %collective-permute-start.13 = (bf16[3,256,3072]{2,1,0:T(8,128)(2,1)}, bf16[3,256,3072]{2,1,0:T(8,128)(2,1)}, u32[]{:S(2)}, u32[]{:S(2)}) collective-permute-start(bf16[3,256,3072]{2,1,0:T(8,128)(2,1)} %x0.1), channel_id=1, source_target_pairs={{0,1},{1,0},{2,3},{3,2},{4,5},{5,4},{6,7},{7,6}} | collective-permute-start | bytes 14155784 | tf_op jit(solution)/shard_map/ppermute | solution.py:342
  54.6 132.7 %copy-start.2 = (bf16[1,256,3072]{2,1,0:T(8,128)(2,1)}, bf16[1,256,3072]{2,1,0:T(8,128)(2,1)S(1)}, u32[]{:S(2)}) copy-start(bf16[1,256,3072]{2,1,0:T(8,128)(2,1)S(1)} %collective-permute-done.4.x0) | copy-start | bytes 4718596
  54.6 157.8 %collective-permute-start = (bf16[1,256,3072]{2,1,0:T(8,128)(2,1)}, bf16[1,256,3072]{2,1,0:T(8,128)(2,1)}, u32[]{:S(2)}, u32[]{:S(2)}) collective-permute-start(bf16[1,256,3072]{2,1,0:T(8,128)(2,1)} %get-tuple-element.80), channel_id=1, source_target_pairs={{0,2},{1,3},{2,0},{3,1},{4,6},{5,7},{6,4},{7,5}} | collective-permute-start | bytes 4718600 | tf_op jit(solution)/shard_map/ppermute | solution.py:343
  88.3 124.1 %copy-start.1 = (bf16[1,256,3072]{2,1,0:T(8,128)(2,1)}, bf16[1,256,3072]{2,1,0:T(8,128)(2,1)S(1)}, u32[]{:S(2)}) copy-start(bf16[1,256,3072]{2,1,0:T(8,128)(2,1)S(1)} %collective-permute-done.2.x0) | copy-start | bytes 4718596
  88.3 124.2 %collective-permute-start.9 = (bf16[1,256,3072]{2,1,0:T(8,128)(2,1)}, bf16[1,256,3072]{2,1,0:T(8,128)(2,1)}, u32[]{:S(2)}, u32[]{:S(2)}) collective-permute-start(bf16[1,256,3072]{2,1,0:T(8,128)(2,1)} %get-tuple-element.76), channel_id=1, source_target_pairs={{0,2},{1,3},{2,0},{3,1},{4,6},{5,7},{6,4},{7,5}} | collective-permute-start | bytes 4718600 | tf_op jit(solution)/shard_map/ppermute | solution.py:344
  122.1 100.9 %collective-permute-start.7 = (bf16[1,256,3072]{2,1,0:T(8,128)(2,1)}, bf16[1,256,3072]{2,1,0:T(8,128)(2,1)}, u32[]{:S(2)}, u32[]{:S(2)}) collective-permute-start(bf16[1,256,3072]{2,1,0:T(8,128)(2,1)} %get-tuple-element.77), channel_id=1, source_target_pairs={{0,2},{1,3},{2,0},{3,1},{4,6},{5,7},{6,4},{7,5}} | collective-permute-start | bytes 4718600 | tf_op jit(solution)/shard_map/ppermute | solution.py:344
  124.1 98.9 %collective-permute-start.5 = (bf16[1,256,3072]{2,1,0:T(8,128)(2,1)S(1)}, bf16[1,256,3072]{2,1,0:T(8,128)(2,1)}, u32[]{:S(2)}, u32[]{:S(2)}) collective-permute-start(bf16[1,256,3072]{2,1,0:T(8,128)(2,1)S(1)} %collective-permute-done.4.x0), channel_id=1, source_target_pairs={{0,1},{1,0},{2,3},{3,2},{4,5},{5,4},{6,7},{7,6}} | collective-permute-start | bytes 4718600 | tf_op jit(solution)/shard_map/ppermute | solution.py:349
  187.2 60.0 %collective-permute-start.12 = (bf16[1,256,3072]{2,1,0:T(8,128)(2,1)}, bf16[1,256,3072]{2,1,0:T(8,128)(2,1)}, u32[]{:S(2)}, u32[]{:S(2)}) collective-permute-start(bf16[1,256,3072]{2,1,0:T(8,128)(2,1)} %collective-permute-done.11.x0), channel_id=1, source_target_pairs={{0,1},{1,0},{2,3},{3,2},{4,5},{5,4},{6,7},{7,6}} | collective-permute-start | bytes 4718600 | tf_op jit(solution)/shard_map/ppermute | solution.py:350
  212.4 45.9 %collective-permute-start.3 = (bf16[1,256,3072]{2,1,0:T(8,128)(2,1)S(1)}, bf16[1,256,3072]{2,1,0:T(8,128)(2,1)}, u32[]{:S(2)}, u32[]{:S(2)}) collective-permute-start(bf16[1,256,3072]{2,1,0:T(8,128)(2,1)S(1)} %collective-permute-done.2.x0), channel_id=1, source_target_pairs={{0,1},{1,0},{2,3},{3,2},{4,5},{5,4},{6,7},{7,6}} | collective-permute-start | bytes 4718600 | tf_op jit(solution)/shard_map/ppermute | solution.py:349
  212.5 70.2 %collective-permute-start.1 = (bf16[1,256,3072]{2,1,0:T(8,128)(2,1)}, bf16[1,256,3072]{2,1,0:T(8,128)(2,1)}, u32[]{:S(2)}, u32[]{:S(2)}) collective-permute-start(bf16[1,256,3072]{2,1,0:T(8,128)(2,1)} %collective-permute-done.x0), channel_id=1, source_target_pairs={{0,1},{1,0},{2,3},{3,2},{4,5},{5,4},{6,7},{7,6}} | collective-permute-start | bytes 4718600 | tf_op jit(solution)/shard_map/ppermute | solution.py:349
  223.0 165.4 %collective-permute-start.10 = (bf16[1,256,3072]{2,1,0:T(8,128)(2,1)}, bf16[1,256,3072]{2,1,0:T(8,128)(2,1)}, u32[]{:S(2)}, u32[]{:S(2)}) collective-permute-start(bf16[1,256,3072]{2,1,0:T(8,128)(2,1)} %collective-permute-done.9.x0), channel_id=1, source_target_pairs={{0,1},{1,0},{2,3},{3,2},{4,5},{5,4},{6,7},{7,6}} | collective-permute-start | bytes 4718600 | tf_op jit(solution)/shard_map/ppermute | solution.py:350
  223.0 258.7 %collective-permute-start.8 = (bf16[1,256,3072]{2,1,0:T(8,128)(2,1)}, bf16[1,256,3072]{2,1,0:T(8,128)(2,1)}, u32[]{:S(2)}, u32[]{:S(2)}) collective-permute-start(bf16[1,256,3072]{2,1,0:T(8,128)(2,1)} %collective-permute-done.7.x0), channel_id=1, source_target_pairs={{0,1},{1,0},{2,3},{3,2},{4,5},{5,4},{6,7},{7,6}} | collective-permute-start | bytes 4718600 | tf_op jit(solution)/shard_map/ppermute | solution.py:350
  616.7 168.2 %collective-permute-start.19 = (f32[1536,3072]{1,0:T(8,128)}, f32[1536,3072]{1,0:T(8,128)}, u32[]{:S(2)}, u32[]{:S(2)}) collective-permute-start(f32[1536,3072]{1,0:T(8,128)} %get-tuple-element.65), channel_id=1, source_target_pairs={{0,1},{1,0},{2,3},{3,2},{4,5},{5,4},{6,7},{7,6}} | collective-permute-start | bytes 56623112 | tf_op jit(solution)/shard_map/ppermute | solution.py:371
  654.5 130.5 %collective-permute-start.16 = (f32[3072,1536]{1,0:T(8,128)}, f32[3072,1536]{1,0:T(8,128)}, u32[]{:S(2)}, u32[]{:S(2)}) collective-permute-start(f32[3072,1536]{1,0:T(8,128)} %get-tuple-element.59), channel_id=1, source_target_pairs={{0,1},{1,0},{2,3},{3,2},{4,5},{5,4},{6,7},{7,6}} | collective-permute-start | bytes 56623112 | tf_op jit(solution)/shard_map/ppermute | solution.py:383
  692.8 92.2 %collective-permute-start.17 = (f32[3072,1536]{1,0:T(8,128)}, f32[3072,1536]{1,0:T(8,128)}, u32[]{:S(2)}, u32[]{:S(2)}) collective-permute-start(f32[3072,1536]{1,0:T(8,128)} %get-tuple-element.61), channel_id=1, source_target_pairs={{0,1},{1,0},{2,3},{3,2},{4,5},{5,4},{6,7},{7,6}} | collective-permute-start | bytes 56623112 | tf_op jit(solution)/shard_map/ppermute | solution.py:383
  730.7 54.2 %collective-permute-start.18 = (f32[3072,1536]{1,0:T(8,128)}, f32[3072,1536]{1,0:T(8,128)}, u32[]{:S(2)}, u32[]{:S(2)}) collective-permute-start(f32[3072,1536]{1,0:T(8,128)} %get-tuple-element.63), channel_id=1, source_target_pairs={{0,1},{1,0},{2,3},{3,2},{4,5},{5,4},{6,7},{7,6}} | collective-permute-start | bytes 56623112 | tf_op jit(solution)/shard_map/ppermute | solution.py:383
  733.1 29.5 %collective-permute-start.14 = (bf16[3,256,1536]{2,1,0:T(8,128)(2,1)S(1)}, bf16[3,256,1536]{2,1,0:T(8,128)(2,1)S(1)}, u32[]{:S(2)}, u32[]{:S(2)}) collective-permute-start(bf16[3,256,1536]{2,1,0:T(8,128)(2,1)S(1)} %constant_dynamic-slice_fusion.1), channel_id=1, source_target_pairs={{0,1},{1,0},{2,3},{3,2},{4,5},{5,4},{6,7},{7,6}} | collective-permute-start | bytes 7077896 | tf_op jit(solution)/shard_map/ppermute | solution.py:363
  762.6 22.3 %collective-permute-start.15 = (bf16[3,3,256,1536]{3,2,1,0:T(8,128)(2,1)}, bf16[3,3,256,1536]{3,2,1,0:T(8,128)(2,1)}, u32[]{:S(2)}, u32[]{:S(2)}) collective-permute-start(bf16[3,3,256,1536]{3,2,1,0:T(8,128)(2,1)} %constant_dynamic-slice_fusion), channel_id=1, source_target_pairs={{0,1},{1,0},{2,3},{3,2},{4,5},{5,4},{6,7},{7,6}} | collective-permute-start | bytes 21233672 | tf_op jit(solution)/shard_map/ppermute | solution.py:363
  874.3 1.2 collective-permute-start.20
  875.5 8.7 collective-permute-start.21
  (10 other events, 262.4 us)
